TPU v7x, 16 devices: a whole 2x2x2 slice. The times are simulated.
16 devices in a mesh: rep: 1, r: 4 (over y, z), s: 4 (over x, core).
Axes of the slice: x: 2, y: 2, z: 2, core: 2. Of those that a mesh axis runs over, the one named last changes fastest.
Arguments:
- x: bfloat16 [16, 4096, 640], P(('rep', 'r', 's'))
- dy: bfloat16 [16, 4096, 640], P(('rep', 'r', 's'))
- w_gate: bfloat16 [2, 640, 2048], P(None, 's')
- w_up: bfloat16 [2, 640, 2048], P(None, 's')
- w_down: bfloat16 [2, 2048, 640], P(None, 's')
- m_w_gate: float32 [2, 640, 2048], P(None, 's')
- m_w_up: float32 [2, 640, 2048], P(None, 's')
- m_w_down: float32 [2, 2048, 640], P(None, 's')
- v_w_gate: float32 [2, 640, 2048], P(None, 's')
- v_w_up: float32 [2, 640, 2048], P(None, 's')
- v_w_down: float32 [2, 2048, 640], P(None, 's')
Outputs:
- output 1: bfloat16 [2, 640, 2048], P('rep', 's')
- output 2: bfloat16 [2, 640, 2048], P('rep', 's')
- output 3: bfloat16 [2, 2048, 640], P('rep', 's')
- output 4: float32 [2, 640, 2048], P('rep', 's')
- output 5: float32 [2, 640, 2048], P('rep', 's')
- output 6: float32 [2, 2048, 640], P('rep', 's')
- output 7: float32 [2, 640, 2048], P('rep', 's')
- output 8: float32 [2, 640, 2048], P('rep', 's')
- output 9: float32 [2, 2048, 640], P('rep', 's')
All inputs are finite; a program needn't handle non-finite values.
Results may differ from a plain program's by a relative error of at most 0.022.
Values are sent between devices in bfloat16 or wider.
A program may use at most 2 GiB of HBM per device.

v0:
```python
import jax
import jax.numpy as jnp
from jax import lax
from jax.sharding import PartitionSpec as P

NAMES = ("w_gate", "w_up", "w_down")


def matmul(a, w):
    return jnp.dot(a, w, preferred_element_type=jnp.float32).astype(jnp.bfloat16)


def normed(h):
    wide = h.astype(jnp.float32)
    scale = lax.rsqrt(jnp.mean(wide**2, -1, keepdims=True) + 1e-6)
    return (wide * scale).astype(jnp.bfloat16)


def layer(h, w):
    a = normed(h)
    gate = jnp.dot(a, w["w_gate"], preferred_element_type=jnp.float32)
    up = jnp.dot(a, w["w_up"], preferred_element_type=jnp.float32)
    return h + matmul((jax.nn.silu(gate) * up).astype(jnp.bfloat16), w["w_down"])


def adamw(w, m, v, g):
    m = 0.9 * m + 0.1 * g
    v = 0.95 * v + 0.05 * g * g
    step = m * lax.rsqrt(v + 1e-8) + 0.1 * w
    return (w - 0.02 * step).astype(jnp.bfloat16), m, v


def clipped(gradients, sum_of_squares, count):
    factor = jnp.minimum(1.0, 0.5 * lax.rsqrt(sum_of_squares / count + 1e-30))
    return [g * factor for g in gradients]


def solution(mesh):
    def fetched(weights, number):
        return {name: lax.all_gather(w[number], "s", axis=0, tiled=True) for name, w in zip(NAMES, weights, strict=True)}

    def summed(term):
        return lax.psum(lax.psum_scatter(term, "s", scatter_dimension=0, tiled=True), "r")

    def step(x, dy, *arrays):
        weights, m, v = (arrays[i : i + 3] for i in (0, 3, 6))
        layers = weights[0].shape[0]
        h, kept = x[0], []
        for number in range(layers):
            kept.append(h)
            h = layer(h, fetched(weights, number))
        by_h, mine = dy[0], [None] * layers
        for number in reversed(range(layers)):
            _, back = jax.vjp(lambda w, h: layer(h, w), fetched(weights, number), kept[number])
            by_w, by_h = back(by_h)
            mine[number] = [summed(by_w[name]) for name in NAMES]
        gradients = [jnp.stack([mine[number][i] for number in range(layers)]).astype(jnp.float32) for i in range(3)]
        squares = lax.psum(sum(jnp.sum(g * g) for g in gradients), "s")
        gradients = clipped(gradients, squares, lax.psum(1, "s") * sum(g.size for g in gradients))
        new = [adamw(w.astype(jnp.float32), m, v, g) for w, m, v, g in zip(weights, m, v, gradients, strict=True)]
        return tuple(one[which] for which in range(3) for one in new)

    states, cut = P(("rep", "r", "s"), None, None), P(None, "s", None)
    return jax.shard_map(
        step,
        mesh=mesh,
        in_specs=(states, states) + (cut,) * 9,
        out_specs=(P("rep", "s", None),) * 9,
        check_vma=False,
    )
```

profile of v0, /device:TPU:0, one launch (start us, length us, event | category | flops | bytes accessed | tf_op | source)
XLA Modules:
  0.0 618.7 jit_solution(12645436151065069430)
XLA Ops:
  7.2 2.6 fusion.103
  9.8 0.0 all-gather.15.cloned.1.call-start
  9.9 2.5 fusion.102
  12.4 0.0 all-gather.17.cloned.1.call-start
  12.5 1.2 fusion.101
  13.7 0.5 all-gather.21.cloned.1.call-update
  14.3 0.5 all-gather.23.cloned.1.call-update
  14.9 0.5 all-gather.19.cloned.1.call-update
  15.4 7.9 %copy.20 = bf16[1,4096,640]{1,2,0:T(8,128)(2,1)} copy(bf16[1,4096,640]{2,1,0:T(8,128)(2,1)} %param.11) | data formatting | bytes 10485760 | tf_op args[0]
  23.4 3.6 fusion.15
  27.0 8.0 %copy.21 = bf16[1,4096,640]{1,2,0:T(8,128)(2,1)} copy(bf16[1,4096,640]{2,1,0:T(8,128)(2,1)} %param.12) | data formatting | bytes 10485760 | tf_op args[1]
  35.0 1.3 all-gather.13.cloned.1.call-done
  36.3 21.8 %fusion.40 = f32[4096,2048]{1,0:T(8,128)} fusion(bf16[1,4096,640]{1,2,0:T(8,128)(2,1)} %copy.20, f32[4096]{0:T(1024)S(1)} %add_rsqrt_fusion, bf16[1,640,2048]{2,1,0:T(8,128)(2,1)} %all-gather.13.cloned.1.call-done), kind=kOutput, calls=%fused_computation.55 | convolution fusion | flops 10745282560 | bytes 41435136 | tf_op jit(solution)/shard_map/dot_general | solution.py:21
  58.1 3.7 all-gather.15.cloned.1.call-done
  61.8 34.0 %multiply_convert_fusion.1 = (bf16[4096,2048]{1,0:T(8,128)(2,1)}, f32[4096,2048]{1,0:T(8,128)}) fusion(f32[4096,2048]{1,0:T(8,128)} %fusion.40, bf16[1,640,2048]{2,1,0:T(8,128)(2,1)} %all-gather.15.cloned.1.call-done, bf16[1,4096,640]{1,2,0:T(8,128)(2,1)} %copy.20, f32[4096]{0:T(1024)S(1)} %add_rsqrt_fusion), kind=kOutput, calls=%fused_computation.17 | convolution fusion | flops 10795614208 | bytes 91766784 | tf_op jit(solution)/shard_map/dot_general | solution.py:22
  95.8 18.6 %fusion.19 = (f32[4096]{0:T(1024)S(1)}, bf16[4096,640]{0,1:T(8,128)(2,1)}) fusion(bf16[4096,2048]{1,0:T(8,128)(2,1)} %get-tuple-element.30, bf16[1,2048,640]{2,1,0:T(8,128)(2,1)} %all-gather.17.cloned.1.call-done, bf16[1,4096,640]{1,2,0:T(8,128)(2,1)} %copy.20), kind=kOutput, calls=%fused_computation.37 | convolution fusion | flops 10750521344 | bytes 29900800 | tf_op jit(solution)/shard_map/dot_general | solution.py:10
  114.4 19.9 %convolution_convert_fusion.1 = bf16[4096,2048]{1,0:T(8,128)(2,1)} fusion(bf16[1,4096,640]{2,1,0:T(8,128)(2,1)} %param.12, bf16[1,2048,640]{2,1,0:T(8,128)(2,1)} %all-gather.21.cloned.1.call-done), kind=kOutput, calls=%fused_computation.29 | convolution fusion | flops 10745806848 | bytes 24641536 | tf_op jit(solution)/shard_map/transpose(jvp())/dot_general | solution.py:10
  134.3 3.6 all-gather.23.cloned.1.call-done
  137.9 21.8 %fusion.32 = f32[4096,2048]{1,0:T(8,128)} fusion(bf16[4096,640]{0,1:T(8,128)(2,1)} %get-tuple-element.33, f32[4096]{0:T(1024)S(1)} %fusion.89, bf16[1,640,2048]{2,1,0:T(8,128)(2,1)} %all-gather.23.cloned.1.call-done), kind=kOutput, calls=%fused_computation.52 | convolution fusion | flops 10745282560 | bytes 41435136 | tf_op jit(solution)/shard_map/jvp()/dot_general | solution.py:22
  159.7 3.6 all-gather.19.cloned.1.call-done
  163.3 44.7 %fusion.2 = (bf16[4096,2048]{1,0:T(8,128)(2,1)}, f32[4096,2048]{1,0:T(8,128)}) fusion(f32[4096,2048]{1,0:T(8,128)} %fusion.32, bf16[4096,2048]{1,0:T(8,128)(2,1)} %convolution_convert_fusion.1, bf16[1,640,2048]{2,1,0:T(8,128)(2,1)} %all-gather.19.cloned.1.call-done, bf16[4096,640]{0,1:T(8,128)(2,1)} %get-tuple-element.33, f32[4096]{0:T(1024)S(1)} %fusion.89), kind=kOutput, calls=%fused_computation.8 | convolution fusion | flops 10845945856 | bytes 108544000 | tf_op jit(solution)/shard_map/jvp()/dot_general | solution.py:21
  208.0 17.1 %convolution_convert_fusion.3 = bf16[4096,640]{0,1:T(8,128)(2,1)} fusion(bf16[4096,2048]{1,0:T(8,128)(2,1)} %get-tuple-element.34, bf16[1,640,2048]{2,1,0:T(8,128)(2,1)} %all-gather.19.cloned.1.call-done), kind=kOutput, calls=%fused_computation.42 | convolution fusion | flops 10737418240 | bytes 24641536 | tf_op jit(solution)/shard_map/transpose(jvp())/dot_general | solution.py:21
  225.1 25.6 %fusion.21 = (f32[4096]{0:T(1024)S(1)}, bf16[4096,640]{0,1:T(8,128)(2,1)}) fusion(bf16[4096,640]{0,1:T(8,128)(2,1)} %get-tuple-element.33, bf16[4096,640]{0,1:T(8,128)(2,1)} %convolution_convert_fusion.3, bf16[1,640,2048]{2,1,0:T(8,128)(2,1)S(1)} %copy-done.19, bf16[4096,2048]{1,0:T(8,128)(2,1)} %convolution_convert_fusion.1, ...), kind=kOutput, calls=%fused_computation.39 | convolution fusion | flops 10803474432 | bytes 68698112 | tf_op jit(solution)/shard_map/transpose(jvp())/dot_general | solution.py:22
  250.8 11.9 %fusion.26 = bf16[4096,640]{0,1:T(8,128)(2,1)} fusion(bf16[4096,640]{0,1:T(8,128)(2,1)} %get-tuple-element.33, bf16[4096,640]{0,1:T(8,128)(2,1)} %get-tuple-element.37, bf16[1,4096,640]{1,2,0:T(8,128)(2,1)} %copy.21, f32[4096]{0:T(1024)S(1)} %multiply_multiply_fusion.3, f32[4096]{0:T(1024)S(1)} %fusion.89), kind=kLoop, calls=%fused_computation.45 | loop fusion | flops 18350080 | bytes 21004288 | tf_op jit(solution)/shard_map/transpose(jvp())/add_any | solution.py:14
  262.7 19.6 %convolution_convert_fusion.4 = bf16[2048,640]{1,0:T(8,128)(2,1)} fusion(bf16[4096,2048]{1,0:T(8,128)(2,1)} %get-tuple-element.30, bf16[4096,640]{0,1:T(8,128)(2,1)} %fusion.26), kind=kOutput, calls=%fused_computation.71 | convolution fusion | flops 10738728960 | bytes 24641536 | tf_op jit(solution)/shard_map/transpose(jvp())/dot_general | solution.py:10
  282.3 0.0 reduce-scatter.17.cloned.1.call-start
  282.4 27.2 %fusion.45 = bf16[2048,640]{1,0:T(8,128)(2,1)} fusion(bf16[1,4096,640]{2,1,0:T(8,128)(2,1)} %param.12, f32[4096,2048]{1,0:T(8,128)} %fusion.32, f32[4096,2048]{1,0:T(8,128)} %get-tuple-element.35), kind=kOutput, calls=%fused_computation.69 | convolution fusion | flops 10789060608 | bytes 74973184 | tf_op jit(solution)/shard_map/transpose(jvp())/dot_general | solution.py:10
  309.6 18.8 %convolution_convert_fusion = bf16[4096,2048]{1,0:T(8,128)(2,1)} fusion(bf16[4096,640]{0,1:T(8,128)(2,1)} %fusion.26, bf16[1,2048,640]{2,1,0:T(8,128)(2,1)S(1)} %copy-done.18), kind=kOutput, calls=%fused_computation.28 | convolution fusion | flops 10745806848 | bytes 24641536 | tf_op jit(solution)/shard_map/transpose(jvp())/dot_general | solution.py:10
  328.4 22.4 %fusion.56 = bf16[640,2048]{1,0:T(8,128)(2,1)} fusion(bf16[4096,2048]{1,0:T(8,128)(2,1)} %convolution_convert_fusion, f32[4096,2048]{1,0:T(8,128)} %fusion.40, bf16[1,4096,640]{1,2,0:T(8,128)(2,1)} %copy.20, f32[4096]{0:T(1024)S(1)} %copy-done.17), kind=kOutput, calls=%fused_computation.73 | convolution fusion | flops 10796924928 | bytes 58212352 | tf_op jit(solution)/shard_map/transpose(jvp())/dot_general | solution.py:22
  350.9 0.0 reduce-scatter.13.cloned.1.call-start
  350.9 22.4 %fusion.48 = bf16[640,2048]{1,0:T(8,128)(2,1)} fusion(bf16[4096,2048]{1,0:T(8,128)(2,1)} %convolution_convert_fusion.1, bf16[4096,640]{0,1:T(8,128)(2,1)} %get-tuple-element.33, f32[4096]{0:T(1024)S(1)} %copy-done.13, f32[4096,2048]{1,0:T(8,128)} %get-tuple-element.35), kind=kOutput, calls=%fused_computation.70 | convolution fusion | flops 10796924928 | bytes 58212352 | tf_op jit(solution)/shard_map/transpose(jvp())/dot_general | solution.py:22
  373.3 0.0 reduce-scatter.7.cloned.1.call-start
  373.4 35.4 %fusion.51 = bf16[640,2048]{1,0:T(8,128)(2,1)} fusion(f32[4096,2048]{1,0:T(8,128)} %fusion.40, f32[4096,2048]{1,0:T(8,128)} %get-tuple-element.31, bf16[4096,2048]{1,0:T(8,128)(2,1)} %convolution_convert_fusion, bf16[1,4096,640]{1,2,0:T(8,128)(2,1)} %copy.20, f32[4096]{0:T(1024)S(1)} %copy-done.17), kind=kOutput, calls=%fused_computation.72 | convolution fusion | flops 10838867968 | bytes 91766784 | tf_op jit(solution)/shard_map/transpose(jvp())/dot_general | solution.py:21
  408.8 17.1 %fusion.42 = bf16[640,2048]{1,0:T(8,128)(2,1)} fusion(bf16[4096,2048]{1,0:T(8,128)(2,1)} %get-tuple-element.34, bf16[4096,640]{0,1:T(8,128)(2,1)} %get-tuple-element.33, f32[4096]{0:T(1024)S(1)} %copy-done.13), kind=kOutput, calls=%fused_computation.68 | convolution fusion | flops 10745282560 | bytes 24657920 | tf_op jit(solution)/shard_map/transpose(jvp())/dot_general | solution.py:21
  426.1 22.6 %reduce-scatter.7.cloned.1.call-done = bf16[160,2048]{1,0:T(8,128)(2,1)} async-done(((bf16[640,2048]{1,0:T(8,128)(2,1)}), bf16[160,2048]{1,0:T(8,128)(2,1)}) %reduce-scatter.7.cloned.1.call-update) | async-done | bytes 655376 | tf_op jit(solution)/shard_map/reduce_scatter | solution.py:43
  448.8 33.5 %reduce-scatter.9.cloned.1.call-done = bf16[160,2048]{1,0:T(8,128)(2,1)} async-done(((bf16[640,2048]{1,0:T(8,128)(2,1)}), bf16[160,2048]{1,0:T(8,128)(2,1)}) %reduce-scatter.9.cloned.1.call-update) | async-done | bytes 655376 | tf_op jit(solution)/shard_map/reduce_scatter | solution.py:43
  482.3 96.1 %all-reduce.3.cloned.1.call-done = (bf16[1,160,2048]{2,1,0:T(8,128)(2,1)}, bf16[1,160,2048]{2,1,0:T(8,128)(2,1)}, bf16[1,160,2048]{2,1,0:T(8,128)(2,1)}, bf16[1,...) async-done(((bf16[1,160,2048]{2,1,0:T(8,128)(2,1)}, bf16[1,160,2048]{2,1,0:T(8,128)(2,1)}, bf16[1,160,2048]{2,1,0:T(8,128)(2,1)}, ...) | async-done | bytes 3932176 | tf_op jit(solution)/shard_map/psum | solution.py:43
  578.5 2.6 fusion.70
  581.0 2.6 fusion.69
  583.6 2.7 fusion.68
  588.2 7.1 %psum.55 = f32[]{:T(128)} all-reduce(f32[]{:T(128)S(6)} %add.111), channel_id=1, replica_groups=mesh['rep'=1,'r'=4,'s'=4] {'s'}, use_global_device_ids=true, to_apply=%region_18.19 | all-reduce | flops 1 | bytes 8 | tf_op jit(solution)/shard_map/psum | solution.py:58
  596.1 6.1 fusion.76
  602.2 1.3 copy-done.5
  603.6 0.7 copy-done.6
  604.3 0.7 copy-done.7
  605.1 0.1 copy-done.8
  605.2 0.2 copy-done.9
  605.3 6.3 %fusion.67 = (bf16[2,160,2048]{2,1,0:T(8,128)(2,1)}, f32[2,160,2048]{2,1,0:T(8,128)}, f32[2,160,2048]{2,1,0:T(8,128)}, bf16[2,160,2048]{2,1,0:T(8,128)(2,1)}, f3...) fusion(bf16[2,160,2048]{2,1,0:T(8,128)(2,1)S(1)} %copy-done.2, f32[]{:T(128)S(6)} %min_shard_map.3, ...), kind=kLoop, calls=%fused_computation.82 | loop fusion | flops 26214400 | bytes 28835844 | tf_op jit(solution)/shard_map/convert_element_type | solution.py:30
  (62 shorter events, 0.7 us)
Async XLA Ops:
  7.2 5.3 copy-start
  7.2 29.1 %all-gather.13.cloned.1.call-start = ((), (), s32[]{:S(2)}) async-start(), calls=%async_computation.12 | async-start | bytes 3276800 | tf_op jit(solution)/shard_map/all_gather | solution.py:40
  9.8 51.9 %all-gather.15.cloned.1.call-start = ((), (), s32[]{:S(2)}) async-start(), calls=%async_computation.13 | async-start | bytes 3276800 | tf_op jit(solution)/shard_map/all_gather | solution.py:40
  12.4 83.4 %all-gather.17.cloned.1.call-start = ((), (), s32[]{:S(2)}) async-start(), calls=%async_computation.14 | async-start | bytes 3276800 | tf_op jit(solution)/shard_map/all_gather | solution.py:40
  13.7 100.8 %all-gather.21.cloned.1.call-start = ((), (), s32[]{:S(2)}) async-start(), calls=%async_computation.16 | async-start | bytes 3276800 | tf_op jit(solution)/shard_map/all_gather | solution.py:40
  14.2 123.7 %all-gather.23.cloned.1.call-start = ((), (), s32[]{:S(2)}) async-start(), calls=%async_computation.17 | async-start | bytes 3276800 | tf_op jit(solution)/shard_map/all_gather | solution.py:40
  14.8 148.4 %all-gather.19.cloned.1.call-start = ((), (), s32[]{:S(2)}) async-start(), calls=%async_computation.15 | async-start | bytes 3276800 | tf_op jit(solution)/shard_map/all_gather | solution.py:40
  15.4 410.6 %reduce-scatter.15.cloned.1.call-start = ((), (), s32[]{:S(2)}) async-start(), calls=%async_computation.10 | async-start | bytes 3276800 | tf_op jit(solution)/shard_map/reduce_scatter | solution.py:43
  27.0 34.8 %copy-start.16 = (f32[4096]{0:T(1024)}, f32[4096]{0:T(1024)S(1)}, u32[]{:S(2)}) copy-start(f32[4096]{0:T(1024)S(1)} %add_rsqrt_fusion) | copy-start | bytes 49156
  114.4 19.9 %copy-start.14 = (f32[4096]{0:T(1024)}, f32[4096]{0:T(1024)S(1)}, u32[]{:S(2)}) copy-start(f32[4096]{0:T(1024)S(1)} %get-tuple-element.32) | copy-start | bytes 49156
  114.4 136.4 %copy-start.12 = (f32[4096]{0:T(1024)}, f32[4096]{0:T(1024)S(1)}, u32[]{:S(2)}) copy-start(f32[4096]{0:T(1024)S(1)} %fusion.89) | copy-start | bytes 49156
  208.0 17.1 %copy-start.19 = (bf16[1,640,2048]{2,1,0:T(8,128)(2,1)S(1)}, bf16[1,640,2048]{2,1,0:T(8,128)(2,1)}, u32[]{:S(2)}) copy-start(bf16[1,640,2048]{2,1,0:T(8,128)(2,1)} %all-gather.23.cloned.1.call-done) | copy-start | bytes 7864324
  225.1 25.6 %copy-start.15 = (f32[4096]{0:T(1024)S(1)}, f32[4096]{0:T(1024)}, u32[]{:S(2)}) copy-start(f32[4096]{0:T(1024)} %copy-done.14) | copy-start | bytes 49156
  282.3 27.3 %copy-start.18 = (bf16[1,2048,640]{2,1,0:T(8,128)(2,1)S(1)}, bf16[1,2048,640]{2,1,0:T(8,128)(2,1)}, u32[]{:S(2)}) copy-start(bf16[1,2048,640]{2,1,0:T(8,128)(2,1)} %all-gather.17.cloned.1.call-done) | copy-start | bytes 7864324
  282.3 143.8 %reduce-scatter.17.cloned.1.call-start = ((), (), s32[]{:S(2)}) async-start(), calls=%async_computation.11 | async-start | bytes 3276800 | tf_op jit(solution)/shard_map/reduce_scatter | solution.py:43
  309.6 18.9 %copy-start.17 = (f32[4096]{0:T(1024)S(1)}, f32[4096]{0:T(1024)}, u32[]{:S(2)}) copy-start(f32[4096]{0:T(1024)} %copy-done.16) | copy-start | bytes 49156
  309.6 116.5 %reduce-scatter.11.cloned.1.call-start = ((), (), s32[]{:S(2)}) async-start(), calls=%async_computation.8 | async-start | bytes 3276800 | tf_op jit(solution)/shard_map/reduce_scatter | solution.py:43
  328.4 22.5 %copy-start.13 = (f32[4096]{0:T(1024)S(1)}, f32[4096]{0:T(1024)}, u32[]{:S(2)}) copy-start(f32[4096]{0:T(1024)} %copy-done.12) | copy-start | bytes 49156
  350.9 75.2 %reduce-scatter.13.cloned.1.call-start = ((), (), s32[]{:S(2)}) async-start(), calls=%async_computation.9 | async-start | bytes 3276800 | tf_op jit(solution)/shard_map/reduce_scatter | solution.py:43
  373.3 75.4 %reduce-scatter.7.cloned.1.call-start = ((), (), s32[]{:S(2)}) async-start(), calls=%async_computation.6 | async-start | bytes 3276800 | tf_op jit(solution)/shard_map/reduce_scatter | solution.py:43
  408.8 73.5 %reduce-scatter.9.cloned.1.call-start = ((), (), s32[]{:S(2)}) async-start(), calls=%async_computation.7 | async-start | bytes 3276800 | tf_op jit(solution)/shard_map/reduce_scatter | solution.py:43
  425.9 170.0 %copy-start.1 = (bf16[2,512,640]{2,1,0:T(8,128)(2,1)S(1)}, bf16[2,512,640]{2,1,0:T(8,128)(2,1)}, u32[]{:S(2)}) copy-start(bf16[2,512,640]{2,1,0:T(8,128)(2,1)} %param.15) | copy-start | bytes 3932164
  426.0 152.5 %all-reduce.3.cloned.1.call-start = ((), (), s32[]{:S(2)}) async-start(), calls=%async_computation.18 | async-start | bytes 7864320 | tf_op jit(solution)/shard_map/psum | solution.py:43
  583.6 18.6 %copy-start.10 = (bf16[1,160,2048]{2,1,0:T(8,128)(2,1)S(1)}, bf16[1,160,2048]{2,1,0:T(8,128)(2,1)}, u32[]{:S(2)}) copy-start(bf16[1,160,2048]{2,1,0:T(8,128)(2,1)} %get-tuple-element.11) | copy-start | bytes 1966084
  583.6 18.6 %copy-start.11 = (bf16[1,160,2048]{2,1,0:T(8,128)(2,1)S(1)}, bf16[1,160,2048]{2,1,0:T(8,128)(2,1)}, u32[]{:S(2)}) copy-start(bf16[1,160,2048]{2,1,0:T(8,128)(2,1)} %get-tuple-element.12) | copy-start | bytes 1966084
  596.0 6.2 %copy-start.2 = (bf16[2,160,2048]{2,1,0:T(8,128)(2,1)S(1)}, bf16[2,160,2048]{2,1,0:T(8,128)(2,1)}, u32[]{:S(2)}) copy-start(bf16[2,160,2048]{2,1,0:T(8,128)(2,1)} %param.13) | copy-start | bytes 3932164
  596.0 6.2 %copy-start.3 = (bf16[2,160,2048]{2,1,0:T(8,128)(2,1)S(1)}, bf16[2,160,2048]{2,1,0:T(8,128)(2,1)}, u32[]{:S(2)}) copy-start(bf16[2,160,2048]{2,1,0:T(8,128)(2,1)} %param.14) | copy-start | bytes 3932164
  596.0 6.2 %copy-start.4 = (f32[2,160,2048]{2,1,0:T(8,128)S(1)}, f32[2,160,2048]{2,1,0:T(8,128)}, u32[]{:S(2)}) copy-start(f32[2,160,2048]{2,1,0:T(8,128)} %param.19) | copy-start | bytes 7864324
  596.0 7.6 %copy-start.5 = (f32[2,160,2048]{2,1,0:T(8,128)S(1)}, f32[2,160,2048]{2,1,0:T(8,128)}, u32[]{:S(2)}) copy-start(f32[2,160,2048]{2,1,0:T(8,128)} %param.16) | copy-start | bytes 7864324
  596.0 8.3 %copy-start.6 = (f32[2,160,2048]{2,1,0:T(8,128)S(1)}, f32[2,160,2048]{2,1,0:T(8,128)}, u32[]{:S(2)}) copy-start(f32[2,160,2048]{2,1,0:T(8,128)} %param.20) | copy-start | bytes 7864324
  596.1 9.0 %copy-start.7 = (f32[2,160,2048]{2,1,0:T(8,128)S(1)}, f32[2,160,2048]{2,1,0:T(8,128)}, u32[]{:S(2)}) copy-start(f32[2,160,2048]{2,1,0:T(8,128)} %param.17) | copy-start | bytes 7864324
  596.1 9.1 %copy-start.8 = (bf16[1,160,2048]{2,1,0:T(8,128)(2,1)S(1)}, bf16[1,160,2048]{2,1,0:T(8,128)(2,1)}, u32[]{:S(2)}) copy-start(bf16[1,160,2048]{2,1,0:T(8,128)(2,1)} %get-tuple-element.9) | copy-start | bytes 1966084
  596.1 9.3 %copy-start.9 = (bf16[1,160,2048]{2,1,0:T(8,128)(2,1)S(1)}, bf16[1,160,2048]{2,1,0:T(8,128)(2,1)}, u32[]{:S(2)}) copy-start(bf16[1,160,2048]{2,1,0:T(8,128)(2,1)} %get-tuple-element.10) | copy-start | bytes 1966084
Sparse Core Ops, SparseCore 0:
  10.1 26.1 all-gather.12
  38.4 23.3 all-gather.14
  63.9 23.3 all-gather.16
  89.2 23.3 all-gather.20
  114.6 23.3 all-gather.22
  139.9 23.3 all-gather.18
  282.4 30.5 reduce-scatter.14
  316.1 30.5 reduce-scatter.16
  351.0 30.5 reduce-scatter.10
  384.5 30.5 reduce-scatter.12
  418.2 30.5 reduce-scatter.6
  451.7 30.5 reduce-scatter.8
  486.2 92.2 all-reduce.2
where the time goes:
time: 626 us; the launch traced here: 619 us
  matrix products  366 us (58%)
  waiting for transfers between devices  166 us (27%)
  other arithmetic  35.7 us (6%)
  local copies, waits for them, and re-layouts  25.4 us (4%)
  between operations  17.3 us (3%)
  blocking collectives  7.09 us (1%)
    dot_general x5, matrix products, layer(): gate = jnp.dot(a, w['w_gate'], preferred_element_type=jnp.float32)  136 us
    dot_general x5, matrix products, layer(): up = jnp.dot(a, w['w_up'], preferred_element_type=jnp.float32)  126 us
    dot_general x5, matrix products, matmul(): jnp.dot(a, w, preferred_element_type=jnp.float32).astype(jnp.bfloat16)  104 us
    psum x1, waiting for transfers between devices, summed(): lax.psum(lax.psum_scatter(term, 's', scatter_dimension=0, tiled=True), 'r')  96.1 us
    reduce_scatter x6, waiting for transfers between devices, summed(): lax.psum_scatter(term, 's', scatter_dimension=0, tiled=True)  56.2 us
    unnamed x42, local copies, waits for them, and re-layouts  19.1 us
  transfers between devices with their start and end apart: 13, of which 7 were waited for; matrix products, arithmetic and copies ran while one was open for 46% of the time, Pallas kernels for 0%

commit v1 on v0

v1 whole, which is shorter than its diff:
```python
import jax
import jax.numpy as jnp
from jax import lax
from jax.experimental import pallas as pl
from jax.experimental.pallas import tpu as pltpu
from jax.sharding import PartitionSpec as P

D, FF, TOK = 640, 2048, 4096
C, F, T = 4, 512, 1024
NT = TOK // T
STEPS = C * NT
RG, RD = 160, 128
EARLY = 6
f32, bf16 = jnp.float32, jnp.bfloat16
MESH = pl.DeviceIdType.MESH
VMEM = pl.BlockSpec(memory_space=pltpu.VMEM)
ANY = pl.BlockSpec(memory_space=pl.ANY)
DMA = pltpu.SemaphoreType.DMA


def dg(a, b, ca, cb):
    return lax.dot_general(a, b, (((ca,), (cb,)), ((), ())), preferred_element_type=f32)


def sigmoid(g):
    return 0.5 * jnp.tanh(0.5 * g) + 0.5


def tile(t):
    return pl.ds(pl.multiple_of(t * T, T), T)


def rows(s, n):
    return pl.ds(pl.multiple_of(s * n, n), n)


def scale_of(wide):
    return lax.rsqrt(jnp.mean(wide * wide, 0, keepdims=True) + 1e-6)


class Place:
    def __init__(self):
        r, self.s = lax.axis_index("r"), lax.axis_index("s")
        self.chip, self.k = self.s // 2, self.s % 2
        y, z = r // 2, r % 2
        self.x_s = 2 * (1 - self.chip) + self.k
        self.core = {"s": 2 * self.chip + 1 - self.k}
        self.x = {"s": self.x_s}
        self.diag = {"s": 2 * (1 - self.chip) + 1 - self.k}
        self.y = {"r": 2 * (1 - y) + z}
        self.z = {"r": 2 * y + 1 - z}


def greet(peers):
    barrier = pltpu.get_barrier_semaphore()
    for peer in peers:
        pl.semaphore_signal(barrier, inc=1, device_id=peer, device_id_type=MESH)
    pl.semaphore_wait(barrier, len(peers))


def remote(src, dst, send, recv, peer):
    return pltpu.make_async_remote_copy(
        src_ref=src, dst_ref=dst, send_sem=send, recv_sem=recv, device_id=peer, device_id_type=MESH
    )


class Gather:
    def __init__(self, at, full, shards, own, sems):
        self.at, self.full, self.shards, self.own, self.sems = at, full, shards, own, sems

    def slot(self, m, u, s):
        return self.full[m].at[u, rows(s, RG if m < 2 else RD), :]

    def fetch(self, u, layer, c):
        for m in range(3):
            if m < 2:
                for q in range(4):
                    pltpu.make_async_copy(
                        self.shards[m].at[layer, :, pl.ds(q * F + c * 128, 128)],
                        self.full[m].at[u, rows(self.at.s, RG), pl.ds(q * 128, 128)],
                        self.own.at[u, m],
                    ).start()
            else:
                pltpu.make_async_copy(self.shards[m].at[layer, pl.ds(c * RD, RD), :], self.slot(m, u, self.at.s), self.own.at[u, m]).start()

    def copy(self, kind, m, u):
        s = self.at.x_s if kind == 2 else self.at.s
        slot = self.slot(m, u, s)
        return remote(slot, slot, self.sems.at[0, kind, u, m], self.sems.at[1, kind, u, m], self.at.x if kind == 0 else self.at.core)

    def send(self, u):
        for m in range(3):
            slot = self.slot(m, u, self.at.s)
            pltpu.make_async_copy(slot, slot, self.own.at[u, m]).wait()
            self.copy(0, m, u).start()
            self.copy(1, m, u).start()

    def forward(self, u):
        for m in range(3):
            self.copy(0, m, u).wait_recv()
            self.copy(2, m, u).start()

    def ready(self, u):
        for m in range(3):
            self.copy(1, m, u).wait_recv()
            self.copy(2, m, u).wait_recv()

    def finish(self, u):
        for m in range(3):
            for kind in range(3):
                self.copy(kind, m, u).wait_send()


def gather_scratch(units):
    return [
        pltpu.VMEM((units, D, F), bf16),
        pltpu.VMEM((units, D, F), bf16),
        pltpu.VMEM((units, F, D), bf16),
        DMA((units, 3)),
        DMA((2, 3, units, 3)),
    ]


class Reduce:
    def __init__(self, at, acc, refs):
        self.at, self.acc = at, acc
        self.p, self.r1, self.b, self.r2, self.q, self.r3, self.q2, self.r4 = (refs[3 * i : 3 * i + 3] for i in range(8))
        self.ss, self.rs = refs[24:]

    def term(self, m, slot, s):
        if m < 2:
            return self.acc[m][slot, rows(s, RG), :]
        return self.acc[2][slot, :, rows(s, RD)].T

    def half(self, m, n):
        h = (RG if m < 2 else RD) // 2
        return pl.ds(n * h, h)

    def copies(self, stage, m, u):
        at = self.at
        if stage == 0:
            return [remote(self.p[m], self.r1[m].at[u], self.ss.at[0, m], self.rs.at[u, 0, m], at.core)]
        if stage == 1:
            return [remote(self.b[m], self.r2[m].at[u], self.ss.at[1, m], self.rs.at[u, 1, m], at.x)]
        src, dst, ways = (self.q, self.r3, (at.y, at.z)) if stage == 2 else (self.q2, self.r4, (at.z, at.y))
        return [
            remote(src[m].at[self.half(m, n)], dst[m].at[u, self.half(m, n)], self.ss.at[2 * stage - 2 + n, m], self.rs.at[u, 2 * stage - 2 + n, m], ways[n])
            for n in range(2)
        ]

    def start(self, stage, m, u):
        for copy in self.copies(stage, m, u):
            copy.start()

    def wait(self, stage, m, u):
        for copy in self.copies(stage, m, u):
            copy.wait()

    def to_core(self, u, slot):
        for m in range(3):
            for j in range(2):
                self.p[m][j] = self.term(m, slot, 2 * j + 1 - self.at.k).astype(bf16)
            self.start(0, m, u)

    def to_x(self, u, slot):
        at = self.at
        for m in range(3):
            self.wait(0, m, u)
            self.b[m][...] = (self.term(m, slot, at.x_s) + self.r1[m][u, 1 - at.chip].astype(f32)).astype(bf16)
            self.start(1, m, u)

    def to_yz(self, u, slot):
        at = self.at
        for m in range(3):
            self.wait(1, m, u)
            total = self.term(m, slot, at.s) + self.r1[m][u, at.chip].astype(f32) + self.r2[m][u].astype(f32)
            self.q[m][...] = total.astype(bf16)
            self.start(2, m, u)

    def to_zy(self, u):
        for m in range(3):
            self.wait(2, m, u)
            self.q2[m][...] = (self.q[m][...].astype(f32) + self.r3[m][u].astype(f32)).astype(bf16)
            self.start(3, m, u)

    def last(self, u, put):
        for m in range(3):
            self.wait(3, m, u)
            put(m, (self.q2[m][...].astype(f32) + self.r4[m][u].astype(f32)).astype(bf16))


def reduce_scratch(units):
    own = [(RG, F), (RG, F), (RD, D)]
    lead = [(2,), (units, 2), (), (units,), (), (units,), (), (units,)]
    return [pltpu.VMEM(n + shape, bf16) for n in lead for shape in own] + [DMA((6, 3)), DMA((units, 6, 3))]


def put_chunk(out, m, c, value):
    if m < 2:
        for q in range(4):
            out[:, pl.ds(pl.multiple_of(q * F + c * 128, 128), 128)] = value[:, q * 128 : (q + 1) * 128]
    else:
        out[rows(c, RD), :] = value


def forward_kernel(x, sg, su, sd, h1, a0, gout, uout, wg1, wu1, wd1, wd0, acc, gb, ub, sems, wg, wu, wd, own, gsems, osem):
    at = Place()
    w = Gather(at, (wg, wu, wd), (sg, su, sd), own, gsems)
    for u in range(EARLY):
        w.fetch(u, u // C, u % C)
    greet((at.core, at.x))
    for u in range(EARLY):
        w.send(u)

    def pre(t, _):
        xt = x[pl.ds(t * T, T), :].T
        h1[:, tile(t)] = xt
        wide = xt.astype(f32)
        a0[:, tile(t)] = (wide * scale_of(wide)).astype(bf16)
        acc[:, tile(t)] = jnp.zeros((D, T), f32)
        return 0

    lax.fori_loop(0, NT, pre, 0)

    def keep(buf, out, k, i):
        return pltpu.make_async_copy(buf.at[i % 2], out.at[i // NT, :, tile(i % NT)], sems.at[k, i % 2])

    w.forward(0)

    def step(i, _):
        c, t = i // NT, i % NT

        @pl.when(t == 0)
        def _():
            w.ready(c)

        @pl.when(t == NT - 1)
        def _():
            w.forward(c + 1)

        @pl.when(i >= 2)
        def _():
            keep(gb, gout, 0, i).wait()
            keep(ub, uout, 1, i).wait()

        a = a0[:, tile(t)]
        g = dg(wg[c], a, 0, 0)
        u = dg(wu[c], a, 0, 0)
        gb[i % 2] = g
        ub[i % 2] = u
        keep(gb, gout, 0, i).start()
        keep(ub, uout, 1, i).start()
        act = (g * sigmoid(g) * u).astype(bf16)
        acc[:, tile(t)] += dg(wd[c], act, 0, 0)
        return 0

    lax.fori_loop(0, STEPS, step, 0)

    outs = [pltpu.make_async_copy(wd.at[pl.ds(0, C)], wd0, osem.at[0, 0])]
    outs[0].start()

    def post(t, _):
        h1[:, tile(t)] = (h1[:, tile(t)].astype(f32) + acc[:, tile(t)].astype(bf16).astype(f32)).astype(bf16)
        return 0

    lax.fori_loop(0, NT, post, 0)
    for u in range(C, EARLY):
        if u > C:
            w.forward(u)
        w.ready(u)
        for m, (full, out) in enumerate(((wg, wg1), (wu, wu1), (wd, wd1))):
            outs.append(pltpu.make_async_copy(full.at[u], out.at[u - C], osem.at[u - C + 1, m]))
            outs[-1].start()
    for u in range(EARLY):
        w.finish(u)
    for k in range(2):
        keep(gb, gout, 0, STEPS - 2 + k).wait()
        keep(ub, uout, 1, STEPS - 2 + k).wait()
    for out in outs:
        out.wait()


def products(g, u, da):
    s = sigmoid(g)
    sg = g * s
    da = da.astype(bf16).astype(f32)
    return (sg * u).astype(bf16), (da * u * (s + sg * (1.0 - s))).astype(bf16), (da * sg).astype(bf16)


def clear(acc, slot):
    for ref in acc:
        ref[slot] = jnp.zeros((D, F), f32)


def top_kernel(h1, dy, wg1, wu1, wd1, sg, su, sd, dh, gg, gu, gd, rawg, rawu, rawd, *scratch):
    a1, acc, dyb, accg, accu, accd, dsem, lsem, wg, wu, wd, own, gsems, *refs = scratch
    at = Place()
    grads = (accg, accu, accd)
    w = Gather(at, (wg, wu, wd), (sg, su, sd), own, gsems)
    red = Reduce(at, grads, refs)
    early = EARLY - C
    loads = [
        [pltpu.make_async_copy(src.at[u], dst.at[u], lsem.at[u, m]) for m, (src, dst) in enumerate(((wg1, wg), (wu1, wu), (wd1, wd)))]
        for u in range(early)
    ]

    def dy_copy(t):
        return pltpu.make_async_copy(dy.at[tile(t), :], dyb, dsem)

    for copy in loads[0]:
        copy.start()
    dy_copy(0).start()
    for u in range(early, C):
        w.fetch(u, 1, u)
    for load in loads[1:]:
        for copy in load:
            copy.start()
    greet((at.core, at.x, at.y, at.z))
    for u in range(early, C):
        w.send(u)

    def pre(t, _):
        wide = h1[:, tile(t)].astype(f32)
        a1[:, tile(t)] = (wide * scale_of(wide)).astype(bf16)
        acc[:, tile(t)] = jnp.zeros((D, T), f32)
        return 0

    lax.fori_loop(0, NT, pre, 0)
    for load in loads:
        for copy in load:
            copy.wait()

    outs = (gg, gu, gd)

    def step(i, _):
        c, t = i // NT, i % NT
        slot = c % 2

        @pl.when((t == 0) & (c >= 2))
        def _():
            red.to_zy(c - 2)

        @pl.when((t == 0) & (c >= 1))
        def _():
            red.to_core(c - 1, 1 - slot)

        @pl.when((t == 1) & (c >= 2))
        def _():
            red.last(c - 2, lambda m, value: put_chunk(outs[m], m, c - 2, value))

        @pl.when((t == 1) & (c >= 1))
        def _():
            red.to_x(c - 1, 1 - slot)

        @pl.when((t == 3) & (c >= 1))
        def _():
            red.to_yz(c - 1, 1 - slot)

        for u in range(early, C):

            @pl.when(i == 2 * (u - early + 1))
            def _():
                w.forward(u)

            @pl.when(i == u * NT)
            def _():
                w.ready(u)

        @pl.when(t == 0)
        def _():
            clear(grads, slot)

        @pl.when(i < NT)
        def _():
            dy_copy(i).wait()
            dh[:, tile(t)] = dyb[...].T

            @pl.when(i + 1 < NT)
            def _():
                dy_copy(i + 1).start()

        a = a1[:, tile(t)]
        y = dh[:, tile(t)]
        g = dg(wg[c], a, 0, 0)
        u = dg(wu[c], a, 0, 0)
        da = dg(wd[c], y, 1, 0)
        act, dgate, dup = products(g, u, da)
        accd[slot] += dg(y, act, 1, 1)
        accg[slot] += dg(a, dgate, 1, 1)
        accu[slot] += dg(a, dup, 1, 1)
        acc[:, tile(t)] += dg(wg[c], dgate, 1, 0) + dg(wu[c], dup, 1, 0)
        return 0

    lax.fori_loop(0, STEPS, step, 0)
    red.to_zy(C - 2)
    raw = [pltpu.make_async_copy(ref.at[(C - 1) % 2], out, lsem.at[0, m]) for m, (ref, out) in enumerate(zip(grads, (rawg, rawu, rawd)))]
    for copy in raw:
        copy.start()

    def post(t, _):
        wide = h1[:, tile(t)].astype(f32)
        scale = scale_of(wide)
        hat = wide * scale
        da = acc[:, tile(t)].astype(bf16).astype(f32)
        da = scale * (da - hat * jnp.mean(da * hat, 0, keepdims=True))
        dh[:, tile(t)] = (dh[:, tile(t)].astype(f32) + da.astype(bf16).astype(f32)).astype(bf16)
        return 0

    lax.fori_loop(0, NT, post, 0)
    red.last(C - 2, lambda m, value: put_chunk(outs[m], m, C - 2, value))
    for u in range(early, C):
        w.finish(u)
    for copy in raw:
        copy.wait()


def squares(value):
    wide = value.astype(f32)
    wide = (wide * wide).reshape(value.shape[0] // 8, 8, value.shape[1]).sum(0)
    return sum(wide[:, n * 128 : (n + 1) * 128] for n in range(value.shape[1] // 128))


def bottom_kernel(a0, dh, wd, gin, uin, rawg, rawu, rawd, gg1, gu1, gd1, gg, gu, gd, total, *scratch):
    accg, accu, accd, gb, ub, sq, everyone, sems, lsem, nsem, *refs = scratch
    at = Place()
    grads = (accg, accu, accd)
    red = Reduce(at, grads, refs)
    raw = [pltpu.make_async_copy(src, ref.at[1], lsem.at[m]) for m, (ref, src) in enumerate(zip(grads, (rawg, rawu, rawd)))]
    for copy in raw:
        copy.start()

    def load(buf, src, k, i):
        return pltpu.make_async_copy(src.at[i // NT, :, tile(i % NT)], buf.at[i % 2], sems.at[k, i % 2])

    load(gb, gin, 0, 0).start()
    load(ub, uin, 1, 0).start()
    greet((at.core, at.x, at.diag, at.y, at.z))
    outs = (gg, gu, gd)
    sq[...] = jnp.zeros((8, 128), f32)
    for out, src in zip(outs, (gg1, gu1, gd1)):
        out[1] = src[...]
    for c in range(C - 1):
        for q in range(4):
            sq[...] += squares(gg1[:, q * F + c * 128 : q * F + (c + 1) * 128]) + squares(gu1[:, q * F + c * 128 : q * F + (c + 1) * 128])
    sq[...] += squares(gd1[: (C - 1) * RD, :])

    def put(u):
        def one(m, value):
            sq[...] += squares(value)
            put_chunk(outs[m].at[jnp.where(u == 0, 1, 0)], m, jnp.where(u == 0, C - 1, u - 1), value)

        return one

    for copy in raw:
        copy.wait()

    def step(i, _):
        c, t = i // NT, i % NT
        slot = c % 2

        @pl.when((t == 0) & (c >= 2))
        def _():
            red.last(c - 2, put(c - 2))

        @pl.when((t == 0) & (c >= 1))
        def _():
            red.to_yz(c - 1, slot)

        @pl.when(t == 0)
        def _():
            red.to_core(c, 1 - slot)
            clear(grads, slot)

        @pl.when(t == 1)
        def _():
            red.to_x(c, 1 - slot)

        @pl.when((t == 2) & (c >= 1))
        def _():
            red.to_zy(c - 1)

        @pl.when(i + 1 < STEPS)
        def _():
            load(gb, gin, 0, i + 1).start()
            load(ub, uin, 1, i + 1).start()

        load(gb, gin, 0, i).wait()
        load(ub, uin, 1, i).wait()
        a = a0[:, tile(t)]
        y = dh[:, tile(t)]
        da = dg(wd[c], y, 1, 0)
        act, dgate, dup = products(gb[i % 2], ub[i % 2], da)
        accd[slot] += dg(y, act, 1, 1)
        accg[slot] += dg(a, dgate, 1, 1)
        accu[slot] += dg(a, dup, 1, 1)
        return 0

    lax.fori_loop(0, STEPS, step, 0)
    red.last(C - 2, put(C - 2))
    red.to_yz(C - 1, 0)
    red.to_core(C, 1)
    red.to_x(C, 1)
    red.to_zy(C - 1)
    red.last(C - 1, put(C - 1))
    red.to_yz(C, 1)
    red.to_zy(C)
    red.last(C, put(C))
    everyone[at.s] = sq[...]
    copies = [
        remote(sq, everyone.at[at.s], nsem.at[0, n], nsem.at[1, n], peer) for n, peer in enumerate((at.core, at.x, at.diag))
    ]
    for copy in copies:
        copy.start()
    for copy in copies:
        copy.wait()
    total[...] = everyone[0] + everyone[1] + everyone[2] + everyone[3]


def adamw_kernel(count, total, *refs):
    mean = jnp.sum(total[...], keepdims=True) / count
    factor = jnp.minimum(1.0, 0.5 * lax.rsqrt(mean + 1e-30))
    for n in range(3):
        g, w, m, v, w_out, m_out, v_out = refs[n::3]
        grad = g[...].astype(f32) * factor.reshape(1, 1, 1)
        m_new = 0.9 * m[...] + 0.1 * grad
        v_new = 0.95 * v[...] + 0.05 * grad * grad
        old = w[...].astype(f32)
        w_out[...] = (old - 0.02 * (m_new * lax.rsqrt(v_new + 1e-8) + 0.1 * old)).astype(bf16)
        m_out[...] = m_new
        v_out[...] = v_new


def params(n):
    return pltpu.CompilerParams(vmem_limit_bytes=66_500_000, collective_id=n, has_side_effects=True)


def cost(matmuls):
    return pl.CostEstimate(flops=matmuls * 2 * D * FF * TOK, bytes_accessed=1 << 26, transcendentals=0)


S = jax.ShapeDtypeStruct


def step(x, dy, *arrays):
    shards, m, v = (arrays[i : i + 3] for i in (0, 3, 6))
    early = EARLY - C
    h1, a0, g, u, wg1, wu1, wd1, wd0 = pl.pallas_call(
        forward_kernel,
        name="forward",
        in_specs=[VMEM] + [ANY] * 3,
        out_specs=[VMEM] * 2 + [ANY] * 6,
        out_shape=[S((D, TOK), bf16)] * 2
        + [S((C, F, TOK), f32)] * 2
        + [S((early, D, F), bf16)] * 2
        + [S((early, F, D), bf16), S((C, F, D), bf16)],
        scratch_shapes=[pltpu.VMEM((D, TOK), f32), pltpu.VMEM((2, F, T), f32), pltpu.VMEM((2, F, T), f32), DMA((2, 2))]
        + gather_scratch(EARLY)
        + [DMA((early + 1, 3))],
        compiler_params=params(0),
        cost_estimate=cost(3),
    )(x[0], *shards)
    dh, gg1, gu1, gd1, *raw = pl.pallas_call(
        top_kernel,
        name="top",
        in_specs=[VMEM] + [ANY] * 7,
        out_specs=[VMEM] * 4 + [ANY] * 3,
        out_shape=[S((D, TOK), bf16), S((RG, FF), bf16), S((RG, FF), bf16), S((C * RD, D), bf16)] + [S((D, F), f32)] * 3,
        scratch_shapes=[
            pltpu.VMEM((D, TOK), bf16),
            pltpu.VMEM((D, TOK), f32),
            pltpu.VMEM((T, D), bf16),
        ]
        + [pltpu.VMEM((2, D, F), f32)] * 3
        + [DMA, DMA((C, 3))]
        + gather_scratch(C)
        + reduce_scratch(C - 1),
        compiler_params=params(1),
        cost_estimate=cost(8),
    )(h1, dy[0], wg1, wu1, wd1, *shards)
    *grads, total = pl.pallas_call(
        bottom_kernel,
        name="bottom",
        in_specs=[VMEM] * 3 + [ANY] * 5 + [VMEM] * 3,
        out_specs=[VMEM] * 4,
        out_shape=[S((2, RG, FF), bf16), S((2, RG, FF), bf16), S((2, C * RD, D), bf16), S((8, 128), f32)],
        scratch_shapes=[pltpu.VMEM((2, D, F), f32)] * 3
        + [
            pltpu.VMEM((2, F, T), f32),
            pltpu.VMEM((2, F, T), f32),
            pltpu.VMEM((8, 128), f32),
            pltpu.VMEM((4, 8, 128), f32),
            DMA((2, 2)),
            DMA((3,)),
            DMA((2, 3)),
        ]
        + reduce_scratch(C + 1),
        compiler_params=params(2),
        cost_estimate=cost(4),
    )(a0, dh, wd0, g, u, *raw, gg1, gu1, gd1)
    blocks = [pl.BlockSpec((1, w.shape[1] // 2, w.shape[2]), lambda l, i: (l, i, 0)) for w in shards]
    count = 4 * sum(w.size for w in shards)
    return pl.pallas_call(
        lambda *refs: adamw_kernel(count, *refs),
        name="adamw",
        grid=(2, 2),
        in_specs=[pl.BlockSpec((8, 128), lambda l, i: (0, 0))] + blocks * 4,
        out_specs=blocks * 3,
        out_shape=[S(w.shape, bf16) for w in shards] + [S(w.shape, f32) for w in shards] * 2,
        compiler_params=pltpu.CompilerParams(vmem_limit_bytes=60_000_000),
        cost_estimate=pl.CostEstimate(flops=40 << 20, bytes_accessed=43 << 20, transcendentals=0),
    )(total, *grads, *shards, *m, *v)


def solution(mesh):
    states, cut = P(("rep", "r", "s"), None, None), P(None, "s", None)
    return jax.shard_map(
        step,
        mesh=mesh,
        in_specs=(states, states) + (cut,) * 9,
        out_specs=(P("rep", "s", None),) * 9,
        check_vma=False,
    )
```

time: 626 us -> 324 us (0.52); the launches traced: 619 us -> 324 us
  matrix products: 366 us -> 0 us
  Pallas kernels: 0 us -> 323 us
  waiting for transfers between devices: 166 us -> 0 us
  other arithmetic: 35.7 us -> 0 us
  local copies, waits for them, and re-layouts: 25.4 us -> 0 us
  between operations: 17.3 us -> 0.84 us
  blocking collectives: 7.09 us -> 0 us
    dot_general x15 -> x0, matrix products: 366 us -> none  [the longest x5 136 us: layer(): gate = jnp.dot(a, w['w_gate'], preferred_element_type=jnp.float32)]
    pallas_call x0 -> x4, Pallas kernels: none -> 323 us  [the longest x1 131 us: step(): pl.pallas_call(top_kernel, name='top', in_specs=[VMEM] + [ANY] * 7, out_s...]
    psum x1 -> x0, waiting for transfers between devices: 96.1 us -> none  [summed(): lax.psum(lax.psum_scatter(term, 's', scatter_dimension=0, tiled=True), 'r')]
    reduce_scatter x6 -> x0, waiting for transfers between devices: 56.2 us -> none  [summed(): lax.psum_scatter(term, 's', scatter_dimension=0, tiled=True)]
    unnamed x42 -> x0, local copies, waits for them, and re-layouts: 19.1 us -> none
    convert_element_type x2 -> x0, other arithmetic: 12.4 us -> none  [adamw(): return ((w - 0.02 * step).astype(jnp.bfloat16), m, v)]
    all_gather x6 -> x0, waiting for transfers between devices: 12.1 us -> none  [fetched(): lax.all_gather(w[number], 's', axis=0, tiled=True)]
    add_any x1 -> x0, other arithmetic: 11.9 us -> none  [normed(): wide = h.astype(jnp.float32)]
  transfers between devices with their start and end apart: 13 -> 0, of which waited for: 7 -> 0; matrix products, arithmetic and copies ran while one was open for 46% -> 0% of each run, Pallas kernels for 0% -> 0%
where the time goes in v1:
time: 324 us
  Pallas kernels  323 us (100%)
    pallas_call x1, Pallas kernels, step(): pl.pallas_call(top_kernel, name='top', in_specs=[VMEM] + [ANY] * 7, out_s...  131 us
    pallas_call x1, Pallas kernels, step(): pl.pallas_call(bottom_kernel, name='bottom', in_specs=[VMEM] * 3 + [ANY]...  98.8 us
    pallas_call x1, Pallas kernels, step(): pl.pallas_call(forward_kernel, name='forward', in_specs=[VMEM] + [ANY] *...  77.1 us
    pallas_call x1, Pallas kernels, step(): pl.pallas_call(lambda *refs: adamw_kernel(count, *refs), name='adamw', gr...  15.5 us

profile of v1, /device:TPU:0, one launch (start us, length us, event | category | flops | bytes accessed | tf_op | source)
XLA Modules:
  0.0 323.5 jit_solution(5476665795648363914)
XLA Ops:
  0.6 77.1 %forward.1 = (bf16[640,4096]{1,0:T(8,128)(2,1)}, bf16[640,4096]{1,0:T(8,128)(2,1)}, f32[4,512,4096]{2,1,0:T(8,128)}, f32[4,512,4096]{2,1,0:T(8,128)}, bf16[2,640...) custom-call(bf16[4096,640]{1,0:T(8,128)(2,1)} %bitcast.2, ...), custom_call_target="tpu_custom_call" | custom-call | flops 32212254720 | bytes 67108864 | tf_op jit(solution)/shard_map/forward/pallas_call | solution.py:547
  77.7 131.3 %top.1 = (bf16[640,4096]{1,0:T(8,128)(2,1)}, bf16[160,2048]{1,0:T(8,128)(2,1)}, bf16[160,2048]{1,0:T(8,128)(2,1)}, bf16[512,640]{1,0:T(8,128)(2,1)}, f32[640,512...) custom-call(bf16[640,4096]{1,0:T(8,128)(2,1)} %get-tuple-element.29.h1, bf16[4096,640]{1,0:T(8,128)(2,1)} %bitcast.3, ...), custom_call_target="tpu_custom_call" | custom-call | flops 85899345920 | bytes 67108864 | tf_op jit(solution)/shard_map/top/pallas_call | solution.py:562
  209.1 98.8 %bottom.1 = (bf16[2,160,2048]{2,1,0:T(8,128)(2,1)}, bf16[2,160,2048]{2,1,0:T(8,128)(2,1)}, bf16[2,512,640]{2,1,0:T(8,128)(2,1)}, f32[8,128]{1,0:T(8,128)}) custom-call(bf16[640,4096]{1,0:T(8,128)(2,1)} %get-tuple-element.28.a0, bf16[640,4096]{1,0:T(8,128)(2,1)} %get-tuple-element.33.dh, bf16[4,512,640]{2,1,0:T(8,128)(2,1)} %get-tuple-element.34.wd, ...), custom_call_target="tpu_custom_call" | custom-call | flops 42949672960 | bytes 67108864 | tf_op jit(solution)/shard_map/bottom/pallas_call | solution.py:580
  307.9 15.5 %adamw.1 = (bf16[2,160,2048]{2,1,0:T(8,128)(2,1)}, bf16[2,160,2048]{2,1,0:T(8,128)(2,1)}, bf16[2,512,640]{2,1,0:T(8,128)(2,1)}, f32[2,160,2048]{2,1,0:T(8,128)},...) custom-call(f32[8,128]{1,0:T(8,128)} %get-tuple-element.43.refs_0_, ...), custom_call_target="tpu_custom_call" | custom-call | flops 41943040 | bytes 45088768 | tf_op jit(solution)/shard_map/adamw/pallas_call | solution.py:602

commit v2 on v1

v2 whole, which is shorter than its diff:
```python
import jax
import jax.numpy as jnp
from jax import lax
from jax.experimental import pallas as pl
from jax.experimental.pallas import tpu as pltpu
from jax.sharding import PartitionSpec as P

D, FF, TOK = 640, 2048, 4096
C, F, T = 4, 512, 1024
NT = TOK // T
STEPS = C * NT
RG, RD = 160, 128
EARLY = 5
f32, bf16 = jnp.float32, jnp.bfloat16
MESH = pl.DeviceIdType.MESH
VMEM = pl.BlockSpec(memory_space=pltpu.VMEM)
ANY = pl.BlockSpec(memory_space=pl.ANY)
DMA = pltpu.SemaphoreType.DMA


def dg(a, b, ca, cb):
    return lax.dot_general(a, b, (((ca,), (cb,)), ((), ())), preferred_element_type=f32)


def sigmoid(g):
    return 0.5 * jnp.tanh(0.5 * g) + 0.5


def tile(t):
    return pl.ds(pl.multiple_of(t * T, T), T)


def rows(s, n):
    return pl.ds(pl.multiple_of(s * n, n), n)


def scale_of(wide):
    return lax.rsqrt(jnp.mean(wide * wide, 0, keepdims=True) + 1e-6)


class Place:
    def __init__(self):
        r, self.s = lax.axis_index("r"), lax.axis_index("s")
        self.chip, self.k = self.s // 2, self.s % 2
        y, z = r // 2, r % 2
        self.x_s = 2 * (1 - self.chip) + self.k
        self.core = {"s": 2 * self.chip + 1 - self.k}
        self.x = {"s": self.x_s}
        self.diag = {"s": 2 * (1 - self.chip) + 1 - self.k}
        self.y = {"r": 2 * (1 - y) + z}
        self.z = {"r": 2 * y + 1 - z}


def greet(peers):
    barrier = pltpu.get_barrier_semaphore()
    for peer in peers:
        pl.semaphore_signal(barrier, inc=1, device_id=peer, device_id_type=MESH)
    pl.semaphore_wait(barrier, len(peers))


def remote(src, dst, send, recv, peer):
    return pltpu.make_async_remote_copy(
        src_ref=src, dst_ref=dst, send_sem=send, recv_sem=recv, device_id=peer, device_id_type=MESH
    )


class Gather:
    def __init__(self, at, full, shards, own, sems):
        self.at, self.full, self.shards, self.own, self.sems = at, full, shards, own, sems

    def slot(self, m, u, s):
        return self.full[m].at[u, rows(s, RD if m else RG), :]

    def fetch(self, u, layer, c):
        for which in range(2):
            for q in range(4):
                pltpu.make_async_copy(
                    self.shards[which].at[layer, :, pl.ds(q * F + c * 128, 128)],
                    self.full[0].at[u, rows(self.at.s, RG), pl.ds(which * F + q * 128, 128)],
                    self.own.at[u, 0],
                ).start()
        pltpu.make_async_copy(self.shards[2].at[layer, pl.ds(c * RD, RD), :], self.slot(1, u, self.at.s), self.own.at[u, 1]).start()

    def copy(self, kind, m, u):
        s = self.at.x_s if kind == 2 else self.at.s
        slot = self.slot(m, u, s)
        return remote(slot, slot, self.sems.at[0, kind, u, m], self.sems.at[1, kind, u, m], self.at.x if kind == 0 else self.at.core)

    def send(self, u):
        for m in range(2):
            slot = self.slot(m, u, self.at.s)
            pltpu.make_async_copy(slot, slot, self.own.at[u, m]).wait()
            self.copy(0, m, u).start()
            self.copy(1, m, u).start()

    def forward(self, u, m):
        self.copy(0, m, u).wait_recv()
        self.copy(2, m, u).start()

    def ready(self, u, m):
        self.copy(1, m, u).wait_recv()
        self.copy(2, m, u).wait_recv()

    def finish(self, u):
        for m in range(2):
            for kind in range(3):
                self.copy(kind, m, u).wait_send()


def gather_scratch(units):
    return [
        pltpu.VMEM((units, D, 2 * F), bf16),
        pltpu.VMEM((units, F, D), bf16),
        DMA((units, 2)),
        DMA((2, 3, units, 2)),
    ]


class Reduce:
    def __init__(self, at, acc, refs):
        self.at, self.acc = at, acc
        self.p, self.r1, self.b, self.r2, self.q, self.r3, self.q2, self.r4, self.own = (refs[3 * i : 3 * i + 3] for i in range(9))
        self.ss, self.rs = refs[27:]

    def term(self, m, slot, s):
        if m < 2:
            return self.acc[0][slot, rows(s, RG), m * F : (m + 1) * F]
        return self.acc[1][slot, :, rows(s, RD)].T

    def half(self, m, n):
        h = (RG if m < 2 else RD) // 2
        return pl.ds(n * h, h)

    def copies(self, stage, m, u):
        at, v = self.at, u % 2
        if stage == 0:
            return [remote(self.p[m], self.r1[m].at[v], self.ss.at[0, m], self.rs.at[v, 0, m], at.core)]
        if stage == 1:
            return [remote(self.b[m], self.r2[m].at[v], self.ss.at[1, m], self.rs.at[v, 1, m], at.x)]
        src, dst, ways = (self.q, self.r3, (at.y, at.z)) if stage == 2 else (self.q2, self.r4, (at.z, at.y))
        return [
            remote(src[m].at[self.half(m, n)], dst[m].at[v, self.half(m, n)], self.ss.at[2 * stage - 2 + n, m], self.rs.at[v, 2 * stage - 2 + n, m], ways[n])
            for n in range(2)
        ]

    def start(self, stage, m, u):
        for copy in self.copies(stage, m, u):
            copy.start()

    def wait(self, stage, m, u):
        for copy in self.copies(stage, m, u):
            copy.wait()

    def to_core(self, u, slot, which=range(3)):
        for m in which:
            for j in range(2):
                self.p[m][j] = self.term(m, slot, 2 * j + 1 - self.at.k).astype(bf16)
            self.start(0, m, u)

    def to_x(self, u, slot, which=range(3)):
        at = self.at
        for m in which:
            self.wait(0, m, u)
            self.b[m][...] = (self.term(m, slot, at.x_s) + self.r1[m][u % 2, 1 - at.chip].astype(f32)).astype(bf16)
            self.start(1, m, u)
        for m in which:
            self.own[m][...] = self.term(m, slot, at.s) + self.r1[m][u % 2, at.chip].astype(f32)

    def to_yz(self, u, which=range(3)):
        for m in which:
            self.wait(1, m, u)
            self.q[m][...] = (self.own[m][...] + self.r2[m][u % 2].astype(f32)).astype(bf16)
            self.start(2, m, u)

    def to_zy(self, u, which=range(3)):
        for m in which:
            self.wait(2, m, u)
            self.q2[m][...] = (self.q[m][...].astype(f32) + self.r3[m][u % 2].astype(f32)).astype(bf16)
            self.start(3, m, u)

    def last(self, u, put, which=range(3)):
        for m in which:
            self.wait(3, m, u)
            put(m, (self.q2[m][...].astype(f32) + self.r4[m][u % 2].astype(f32)).astype(bf16))


def reduce_scratch():
    own = [(RG, F), (RG, F), (RD, D)]
    lead = [(2,), (2, 2), (), (2,), (), (2,), (), (2,)]
    buffers = [pltpu.VMEM(n + shape, bf16) for n in lead for shape in own]
    return buffers + [pltpu.VMEM(shape, f32) for shape in own] + [DMA((6, 3)), DMA((2, 6, 3))]


def put_chunk(out, m, c, value):
    if m < 2:
        for q in range(4):
            out[:, pl.ds(pl.multiple_of(q * F + c * 128, 128), 128)] = value[:, q * 128 : (q + 1) * 128]
    else:
        out[rows(c, RD), :] = value


def forward_kernel(x, dy, sg, su, sd, h1_out, a0_out, dyt_out, gout, uout, wgu1, wd1, wd0, h1, a0, acc, xb, yb, gb, ub, sems, wgu, wd, own, gsems, osem, xsem, ysem):
    at = Place()
    w = Gather(at, (wgu, wd), (sg, su, sd), own, gsems)
    w.fetch(0, 0, 0)
    xs = [pltpu.make_async_copy(x.at[pl.ds(t * T, T), :], xb.at[pl.ds(t * T, T), :], xsem.at[t]) for t in range(NT)]
    xs[0].start()
    greet((at.core, at.x))
    w.send(0)
    for u in range(1, EARLY):
        w.fetch(u, u // C, u % C)
        if u < NT:
            xs[u].start()
    for u in range(1, EARLY):
        w.send(u)

    outs = []
    ys = [pltpu.make_async_copy(dy.at[pl.ds(t * T, T), :], xb.at[pl.ds(t * T, T), :], xsem.at[t]) for t in range(NT)]
    for t in range(NT):
        here = slice(t * T, (t + 1) * T)
        xs[t].wait()
        xt = xb[here, :].T
        h1[:, here] = xt
        wide = xt.astype(f32)
        a0[:, here] = (wide * scale_of(wide)).astype(bf16)
        ys[t].start()
        acc[:, here] = jnp.zeros((D, T), f32)
        outs.append(pltpu.make_async_copy(a0.at[:, pl.ds(t * T, T)], a0_out.at[:, pl.ds(t * T, T)], ysem.at[0, t]))
        outs[-1].start()
    for t in range(NT):
        ys[t].wait()
        yb[:, t * T : (t + 1) * T] = xb[t * T : (t + 1) * T, :].T
        outs.append(pltpu.make_async_copy(yb.at[:, pl.ds(t * T, T)], dyt_out.at[:, pl.ds(t * T, T)], ysem.at[1, t]))
        outs[-1].start()

    def keep(buf, out, k, i):
        return pltpu.make_async_copy(buf.at[i % 2], out.at[i // NT, :, tile(i % NT)], sems.at[k, i % 2])

    for m in range(2):
        w.forward(0, m)
        w.ready(0, m)

    def step(i, _):
        c, t = i // NT, i % NT

        @pl.when((t == 0) & (c >= 1))
        def _():
            w.ready(c, 0)
            w.ready(c, 1)

        @pl.when(t == NT - 1)
        def _():
            w.forward(c + 1, 0)
            w.forward(c + 1, 1)

        @pl.when(i >= 2)
        def _():
            keep(gb, gout, 0, i).wait()
            keep(ub, uout, 1, i).wait()

        both = dg(wgu[c], a0[:, tile(t)], 0, 0)
        g, u = both[:F], both[F:]
        gb[i % 2] = g
        ub[i % 2] = u
        keep(gb, gout, 0, i).start()
        keep(ub, uout, 1, i).start()
        act = (g * sigmoid(g) * u).astype(bf16)

        acc[:, tile(t)] += dg(wd[c], act, 0, 0)
        return 0

    lax.fori_loop(0, STEPS, step, 0)


    outs.append(pltpu.make_async_copy(wd.at[pl.ds(0, C)], wd0, osem.at[0, 0]))
    outs[-1].start()
    for t in range(NT):
        here = slice(t * T, (t + 1) * T)
        h1[:, here] = (h1[:, here].astype(f32) + acc[:, here].astype(bf16).astype(f32)).astype(bf16)
        outs.append(pltpu.make_async_copy(h1.at[:, pl.ds(t * T, T)], h1_out.at[:, pl.ds(t * T, T)], ysem.at[2, t]))
        outs[-1].start()
    for u in range(C, EARLY):
        for m, (full, out) in enumerate(((wgu, wgu1), (wd, wd1))):
            if u > C:
                w.forward(u, m)
            w.ready(u, m)
            outs.append(pltpu.make_async_copy(full.at[u], out.at[u - C], osem.at[u - C + 1, m]))
            outs[-1].start()
    for u in range(EARLY):
        w.finish(u)
    for k in range(2):
        keep(gb, gout, 0, STEPS - 2 + k).wait()
        keep(ub, uout, 1, STEPS - 2 + k).wait()
    for out in outs:
        out.wait()


def products(g, u, da):
    s = sigmoid(g)
    sg = g * s
    da = da.astype(bf16).astype(f32)
    return (sg * u).astype(bf16), (da * u * (s + sg * (1.0 - s))).astype(bf16), (da * sg).astype(bf16)


def clear(acc, slot):
    for ref in acc:
        ref[slot] = jnp.zeros(ref.shape[1:], f32)


def top_kernel(h1_in, dyt, wgu1, wd1, sg, su, sd, dh_out, gg, gu, gd, rawgu, rawd, *scratch):
    h1, dh, a1, acc, scales, dgu, accgu, accd, tsem, lsem, wgu, wd, own, gsems, *refs = scratch
    at = Place()
    grads = (accgu, accd)
    w = Gather(at, (wgu, wd), (sg, su, sd), own, gsems)
    red = Reduce(at, grads, refs)
    early = EARLY - C
    loads = [
        [pltpu.make_async_copy(src.at[u], dst.at[u], lsem.at[u, m]) for m, (src, dst) in enumerate(((wgu1, wgu), (wd1, wd)))]
        for u in range(early)
    ]

    def columns(src, dst, k, t):
        return pltpu.make_async_copy(src.at[:, tile(t)], dst.at[:, tile(t)], tsem.at[k, t])

    columns(h1_in, h1, 0, 0).start()
    for copy in loads[0]:
        copy.start()
    for u in range(early, C):
        w.fetch(u, 1, u)
    for t in range(1, NT):
        columns(h1_in, h1, 0, t).start()
    for t in range(NT):
        columns(dyt, dh, 1, t).start()
    for load in loads[1:]:
        for copy in load:
            copy.start()
    greet((at.core, at.x, at.y, at.z))
    for u in range(early, C):
        w.send(u)

    def pre(t, _):
        columns(h1_in, h1, 0, t).wait()
        wide = h1[:, tile(t)].astype(f32)
        scale = scale_of(wide)
        scales[:, tile(t)] = scale
        a1[:, tile(t)] = (wide * scale).astype(bf16)
        acc[:, tile(t)] = jnp.zeros((D, T), f32)
        return 0

    lax.fori_loop(0, NT, pre, 0)
    for load in loads:
        for copy in load:
            copy.wait()
    for t in range(NT):
        columns(dyt, dh, 1, t).wait()

    outs = (gg, gu, gd)

    def step(i, _):
        c, t = i // NT, i % NT
        slot = c % 2

        @pl.when((t == 0) & (c >= 2))
        def _():
            red.to_zy(c - 2)

        @pl.when((t == 0) & (c >= 1))
        def _():
            red.to_core(c - 1, 1 - slot)

        @pl.when((t == 1) & (c >= 2))
        def _():
            red.last(c - 2, lambda m, value: put_chunk(outs[m], m, c - 2, value))

        @pl.when((t == 1) & (c >= 1))
        def _():
            red.to_x(c - 1, 1 - slot)

        @pl.when((t == 3) & (c >= 1))
        def _():
            red.to_yz(c - 1)

        for u in range(early, C):

            @pl.when(i == 2 * (u - early) + 2)
            def _():
                w.forward(u, 0)
                w.forward(u, 1)

            @pl.when(i == u * NT)
            def _():
                w.ready(u, 0)
                w.ready(u, 1)

        @pl.when(t == 0)
        def _():
            clear(grads, slot)

        a = a1[:, tile(t)]
        y = dh[:, tile(t)]
        both = dg(wgu[c], a, 0, 0)
        act, dgu[:F], dgu[F:] = products(both[:F], both[F:], dg(wd[c], y, 1, 0))
        accd[slot] += dg(y, act, 1, 1)
        accgu[slot] += dg(a, dgu[...], 1, 1)
        acc[:, tile(t)] += dg(wgu[c], dgu[...], 1, 0)
        return 0

    lax.fori_loop(0, STEPS, step, 0)
    red.to_zy(C - 2)
    raw = [pltpu.make_async_copy(ref.at[(C - 1) % 2], out, lsem.at[0, m]) for m, (ref, out) in enumerate(zip(grads, (rawgu, rawd)))]
    for copy in raw:
        copy.start()


    def post(t, _):
        scale = scales[:, tile(t)]
        wide = h1[:, tile(t)].astype(f32)
        da = acc[:, tile(t)].astype(bf16).astype(f32)
        along = scale * scale * scale * jnp.mean(da * wide, 0, keepdims=True)
        dh[:, tile(t)] = (dh[:, tile(t)].astype(f32) + (scale * da - along * wide).astype(bf16).astype(f32)).astype(bf16)
        columns(dh, dh_out, 0, t).start()
        return 0

    lax.fori_loop(0, NT, post, 0)
    red.last(C - 2, lambda m, value: put_chunk(outs[m], m, C - 2, value))
    for u in range(early, C):
        w.finish(u)
    for copy in raw:
        copy.wait()
    for t in range(NT):
        columns(dh, dh_out, 0, t).wait()


def squares(value):
    wide = value.astype(f32)
    wide = (wide * wide).reshape(value.shape[0] // 8, 8, value.shape[1]).sum(0)
    return sum(wide[:, n * 128 : (n + 1) * 128] for n in range(value.shape[1] // 128))


def bottom_kernel(a0_in, dh_in, wd_in, gin, uin, rawgu, rawd, gg1, gu1, gd1, gg_out, gu_out, gd_out, total, *scratch):
    a0, dh, wd, gg, gu, gd, accgu, accd, gb, ub, sq, everyone, sems, lsem, nsem, tsem, fsem, *refs = scratch
    at = Place()
    grads = (accgu, accd)
    red = Reduce(at, grads, refs)
    raw = [pltpu.make_async_copy(src, ref.at[1], lsem.at[m]) for m, (ref, src) in enumerate(zip(grads, (rawgu, rawd)))]

    def load(buf, src, k, i):
        return pltpu.make_async_copy(src.at[i // NT, :, tile(i % NT)], buf.at[i % 2], sems.at[k, i % 2])

    def tiles(t):
        return [
            pltpu.make_async_copy(dh_in.at[:, tile(t)], dh.at[:, tile(t)], tsem.at[0, t]),
            pltpu.make_async_copy(a0_in.at[:, tile(t)], a0.at[:, tile(t)], tsem.at[1, t]),
            pltpu.make_async_copy(wd_in.at[t], wd.at[t], tsem.at[2, t]),
        ]

    outs = (gg, gu, gd)
    done = [pltpu.make_async_copy(src, ref.at[1], fsem.at[0, m]) for m, (ref, src) in enumerate(zip(outs, (gg1, gu1, gd1)))]
    for copy in tiles(0):
        copy.start()
    load(gb, gin, 0, 0).start()
    load(ub, uin, 1, 0).start()
    for copy in tiles(1) + raw + tiles(2) + tiles(3) + done:
        copy.start()
    greet((at.core, at.x, at.diag, at.y, at.z))
    sq[...] = jnp.zeros((8, 128), f32)

    def put(u):
        def one(m, value):
            sq[...] += squares(value)
            put_chunk(outs[m].at[jnp.where(u == 0, 1, 0)], m, jnp.where(u == 0, C - 1, u - 1), value)

        return one

    def step(i, _):
        c, t = i // NT, i % NT
        slot = c % 2

        @pl.when(i < NT)
        def _():
            for copy in tiles(t):
                copy.wait()

        @pl.when(i == 1)
        def _():
            for copy in raw + done:
                copy.wait()

            red.to_core(0, 1)

        @pl.when((t == 0) & (c >= 1))
        def _():
            red.to_core(c, 1 - slot)

        @pl.when(t == 0)
        def _():
            clear(grads, slot)

        @pl.when((t == 1) & (c >= 2))
        def _():
            red.last(c - 2, put(c - 2))

        @pl.when((t == 1) & (c >= 1))
        def _():
            red.to_yz(c - 1)

        @pl.when(((t == 1) & (c >= 1)) | (i == 2))
        def _():
            red.to_x(c, 1 - slot)

        @pl.when((t == 3) & (c >= 1))
        def _():
            red.to_zy(c - 1)

        @pl.when(i + 1 < STEPS)
        def _():
            load(gb, gin, 0, i + 1).start()
            load(ub, uin, 1, i + 1).start()

        load(gb, gin, 0, i).wait()
        load(ub, uin, 1, i).wait()
        a = a0[:, tile(t)]
        y = dh[:, tile(t)]
        da = dg(wd[c], y, 1, 0)
        act, dgate, dup = products(gb[i % 2], ub[i % 2], da)
        accd[slot] += dg(y, act, 1, 1)
        accgu[slot] += dg(a, jnp.concatenate([dgate, dup], 0), 1, 1)
        return 0

    lax.fori_loop(0, STEPS, step, 0)
    red.to_core(C, 1)
    red.last(C - 2, put(C - 2))
    red.to_yz(C - 1)
    red.to_x(C, 1)
    red.to_zy(C - 1)
    for c in range(C - 1):
        for q in range(4):
            sq[...] += squares(gg[1, :, q * F + c * 128 : q * F + (c + 1) * 128]) + squares(gu[1, :, q * F + c * 128 : q * F + (c + 1) * 128])
    sq[...] += squares(gd[1, : (C - 1) * RD, :])
    late = [
        [pltpu.make_async_copy(ref.at[l], out.at[l], fsem.at[1 + l, m]) for m, (ref, out) in enumerate(zip(outs, (gg_out, gu_out, gd_out)))]
        for l in range(2)
    ]
    for copy in late[1]:
        copy.start()
    red.to_yz(C, (0,))
    red.to_yz(C, (1,))
    red.last(C - 1, put(C - 1))
    red.to_zy(C, (0,))
    red.to_yz(C, (2,))
    red.to_zy(C, (1,))
    red.last(C, put(C), (0,))
    red.to_zy(C, (2,))
    red.last(C, put(C), (1,))
    red.last(C, put(C), (2,))
    for copy in late[0]:
        copy.start()
    everyone[at.s] = sq[...]
    copies = [
        remote(sq, everyone.at[at.s], nsem.at[0, n], nsem.at[1, n], peer) for n, peer in enumerate((at.core, at.x, at.diag))
    ]
    for copy in copies:
        copy.start()
    for copy in copies:
        copy.wait()
    total[...] = everyone[0] + everyone[1] + everyone[2] + everyone[3]
    for copy in late[0] + late[1]:
        copy.wait()


def adamw_kernel(count, total, *refs):
    mean = jnp.sum(total[...], keepdims=True) / count
    factor = jnp.minimum(1.0, 0.5 * lax.rsqrt(mean + 1e-30))
    for n in range(3):
        g, w, m, v, w_out, m_out, v_out = refs[n::3]
        grad = g[...].astype(f32) * factor.reshape(1, 1, 1)
        m_new = 0.9 * m[...] + 0.1 * grad
        v_new = 0.95 * v[...] + 0.05 * grad * grad
        old = w[...].astype(f32)
        w_out[...] = (old - 0.02 * (m_new * lax.rsqrt(v_new + 1e-8) + 0.1 * old)).astype(bf16)
        m_out[...] = m_new
        v_out[...] = v_new


def params(n):
    return pltpu.CompilerParams(vmem_limit_bytes=67_000_000, collective_id=n, has_side_effects=True)


def cost(matmuls):
    return pl.CostEstimate(flops=matmuls * 2 * D * FF * TOK, bytes_accessed=1 << 26, transcendentals=0)


S = jax.ShapeDtypeStruct


def step(x, dy, *arrays):
    shards, m, v = (arrays[i : i + 3] for i in (0, 3, 6))
    early = EARLY - C
    h1, a0, dyt, g, u, wgu1, wd1, wd0 = pl.pallas_call(
        forward_kernel,
        name="forward",
        in_specs=[ANY] * 5,
        out_specs=[ANY] * 8,
        out_shape=[S((D, TOK), bf16)] * 3
        + [S((C, F, TOK), f32)] * 2
        + [S((early, D, 2 * F), bf16), S((early, F, D), bf16), S((C, F, D), bf16)],
        scratch_shapes=[pltpu.VMEM((D, TOK), bf16)] * 2
        + [pltpu.VMEM((D, TOK), f32), pltpu.VMEM((TOK, D), bf16), pltpu.VMEM((D, TOK), bf16), pltpu.VMEM((2, F, T), f32), pltpu.VMEM((2, F, T), f32), DMA((2, 2))]
        + gather_scratch(EARLY)
        + [DMA((early + 1, 2)), DMA((NT,)), DMA((3, NT))],
        compiler_params=params(0),
        cost_estimate=cost(3),
    )(x[0], dy[0], *shards)
    dh, gg1, gu1, gd1, *raw = pl.pallas_call(
        top_kernel,
        name="top",
        in_specs=[ANY] * 7,
        out_specs=[ANY] + [VMEM] * 3 + [ANY] * 2,
        out_shape=[S((D, TOK), bf16), S((RG, FF), bf16), S((RG, FF), bf16), S((C * RD, D), bf16)] + [S((D, 2 * F), f32), S((D, F), f32)],
        scratch_shapes=[
            pltpu.VMEM((D, TOK), bf16),
            pltpu.VMEM((D, TOK), bf16),
            pltpu.VMEM((D, TOK), bf16),
            pltpu.VMEM((D, TOK), f32),
            pltpu.VMEM((1, TOK), f32),
            pltpu.VMEM((2 * F, T), bf16),
            pltpu.VMEM((2, D, 2 * F), f32),
            pltpu.VMEM((2, D, F), f32),
        ]
        + [DMA((2, NT)), DMA((C, 2))]
        + gather_scratch(C)
        + reduce_scratch(),
        compiler_params=params(1),
        cost_estimate=cost(8),
    )(h1, dyt, wgu1, wd1, *shards)
    *grads, total = pl.pallas_call(
        bottom_kernel,
        name="bottom",
        in_specs=[ANY] * 10,
        out_specs=[ANY] * 3 + [VMEM],
        out_shape=[S((2, RG, FF), bf16), S((2, RG, FF), bf16), S((2, C * RD, D), bf16), S((8, 128), f32)],
        scratch_shapes=[
            pltpu.VMEM((D, TOK), bf16),
            pltpu.VMEM((D, TOK), bf16),
            pltpu.VMEM((C, F, D), bf16),
            pltpu.VMEM((2, RG, FF), bf16),
            pltpu.VMEM((2, RG, FF), bf16),
            pltpu.VMEM((2, C * RD, D), bf16),
            pltpu.VMEM((2, D, 2 * F), f32),
            pltpu.VMEM((2, D, F), f32),
            pltpu.VMEM((2, F, T), f32),
            pltpu.VMEM((2, F, T), f32),
            pltpu.VMEM((8, 128), f32),
            pltpu.VMEM((4, 8, 128), f32),
            DMA((2, 2)),
            DMA((2,)),
            DMA((2, 3)),
            DMA((3, NT)),
            DMA((3, 3)),
        ]
        + reduce_scratch(),
        compiler_params=params(2),
        cost_estimate=cost(4),
    )(a0, dh, wd0, g, u, *raw, gg1, gu1, gd1)
    blocks = [pl.BlockSpec((1, w.shape[1] // 2, w.shape[2]), lambda l, i: (l, i, 0)) for w in shards]
    count = 4 * sum(w.size for w in shards)
    return pl.pallas_call(
        lambda *refs: adamw_kernel(count, *refs),
        name="adamw",
        grid=(2, 2),
        in_specs=[pl.BlockSpec((8, 128), lambda l, i: (0, 0))] + blocks * 4,
        out_specs=blocks * 3,
        out_shape=[S(w.shape, bf16) for w in shards] + [S(w.shape, f32) for w in shards] * 2,
        compiler_params=pltpu.CompilerParams(vmem_limit_bytes=60_000_000),
        cost_estimate=pl.CostEstimate(flops=40 << 20, bytes_accessed=43 << 20, transcendentals=0),
    )(total, *grads, *shards, *m, *v)


def solution(mesh):
    states, cut = P(("rep", "r", "s"), None, None), P(None, "s", None)
    return jax.shard_map(
        step,
        mesh=mesh,
        in_specs=(states, states) + (cut,) * 9,
        out_specs=(P("rep", "s", None),) * 9,
        check_vma=False,
    )
```

time: 324 us -> 301 us (0.929)
  Pallas kernels: 323 us -> 300 us
    pallas_call x3, Pallas kernels: 307 us -> 285 us  [the longest x1 124 us: step(): pl.pallas_call(top_kernel, name='top', in_specs=[ANY] * 7, out_specs=[ANY...]
where the time goes in v2:
time: 301 us
  Pallas kernels  300 us (100%)
    pallas_call x1, Pallas kernels, step(): pl.pallas_call(top_kernel, name='top', in_specs=[ANY] * 7, out_specs=[ANY...  124 us
    pallas_call x1, Pallas kernels, step(): pl.pallas_call(bottom_kernel, name='bottom', in_specs=[ANY] * 10, out_spe...  94.5 us
    pallas_call x1, Pallas kernels, step(): pl.pallas_call(forward_kernel, name='forward', in_specs=[ANY] * 5, out_sp...  66.2 us
    pallas_call x1, Pallas kernels, step(): pl.pallas_call(lambda *refs: adamw_kernel(count, *refs), name='adamw', gr...  15.2 us

profile of v2, /device:TPU:0, one launch (start us, length us, event | category | flops | bytes accessed | tf_op | source)
XLA Modules:
  0.0 301.0 jit_solution(14244795094705826715)
XLA Ops:
  0.6 66.2 %forward.1 = (bf16[640,4096]{1,0:T(8,128)(2,1)}, bf16[640,4096]{1,0:T(8,128)(2,1)}, bf16[640,4096]{1,0:T(8,128)(2,1)}, f32[4,512,4096]{2,1,0:T(8,128)}, f32[4,51...) custom-call(bf16[4096,640]{1,0:T(8,128)(2,1)} %bitcast.2, ...), custom_call_target="tpu_custom_call" | custom-call | flops 32212254720 | bytes 67108864 | tf_op jit(solution)/shard_map/forward/pallas_call | solution.py:599
  66.9 124.2 %top.1 = (bf16[640,4096]{1,0:T(8,128)(2,1)}, bf16[160,2048]{1,0:T(8,128)(2,1)}, bf16[160,2048]{1,0:T(8,128)(2,1)}, bf16[512,640]{1,0:T(8,128)(2,1)}, f32[640,1024]{1,0:T(8,128)}, /*index=5*/f32[640,512]{1,0:T(8,128)}) custom-call(bf16[640,4096]{1,0:T(8,128)(2,1)} %get-tuple-element.28.h1_in, bf16[640,4096]{1,0:T(8,128)(2,1)} %get-tuple-element.29.dyt, ...), custom_call_target="tpu_custom_call" | custom-call | flops 85899345920 | bytes 67108864 | tf_op jit(solution)/shard_map/top/pallas_call | solution.py:614
  191.1 94.5 %bottom.1 = (bf16[2,160,2048]{2,1,0:T(8,128)(2,1)}, bf16[2,160,2048]{2,1,0:T(8,128)(2,1)}, bf16[2,512,640]{2,1,0:T(8,128)(2,1)}, f32[8,128]{1,0:T(8,128)}) custom-call(bf16[640,4096]{1,0:T(8,128)(2,1)} %get-tuple-element.27.a0_in, bf16[640,4096]{1,0:T(8,128)(2,1)} %get-tuple-element.32.dh_in, bf16[4,512,640]{2,1,0:T(8,128)(2,1)} %get-tuple-element.33.wd_in, ...), custom_call_target="tpu_custom_call" | custom-call | flops 42949672960 | bytes 67108864 | tf_op jit(solution)/shard_map/bottom/pallas_call | solution.py:636
  285.6 15.2 %adamw.1 = (bf16[2,160,2048]{2,1,0:T(8,128)(2,1)}, bf16[2,160,2048]{2,1,0:T(8,128)(2,1)}, bf16[2,512,640]{2,1,0:T(8,128)(2,1)}, f32[2,160,2048]{2,1,0:T(8,128)},...) custom-call(f32[8,128]{1,0:T(8,128)} %get-tuple-element.41.refs_0_, ...), custom_call_target="tpu_custom_call" | custom-call | flops 41943040 | bytes 45088768 | tf_op jit(solution)/shard_map/adamw/pallas_call | solution.py:667

commit v3 on v2

--- a/solution.py
+++ b/solution.py
@@ -43,6 +43,7 @@
         r, self.s = lax.axis_index("r"), lax.axis_index("s")
         self.chip, self.k = self.s // 2, self.s % 2
         y, z = r // 2, r % 2
+        self.y_at = y
         self.x_s = 2 * (1 - self.chip) + self.k
         self.core = {"s": 2 * self.chip + 1 - self.k}
         self.x = {"s": self.x_s}
@@ -65,8 +66,8 @@
 
 
 class Gather:
-    def __init__(self, at, full, shards, own, sems):
-        self.at, self.full, self.shards, self.own, self.sems = at, full, shards, own, sems
+    def __init__(self, at, full, shards, own, sems, shared):
+        self.at, self.full, self.shards, self.own, self.sems, self.shared = at, full, shards, own, sems, shared
 
     def slot(self, m, u, s):
         return self.full[m].at[u, rows(s, RD if m else RG), :]
@@ -81,13 +82,21 @@
                 ).start()
         pltpu.make_async_copy(self.shards[2].at[layer, pl.ds(c * RD, RD), :], self.slot(1, u, self.at.s), self.own.at[u, 1]).start()
 
+    def split(self, m, u):
+        return self.shared and m == 1 and not (isinstance(u, int) and u == 0)
+
     def copy(self, kind, m, u):
-        s = self.at.x_s if kind == 2 else self.at.s
+        at = self.at
+        s = at.x_s if kind >= 2 else at.s
         slot = self.slot(m, u, s)
-        return remote(slot, slot, self.sems.at[0, kind, u, m], self.sems.at[1, kind, u, m], self.at.x if kind == 0 else self.at.core)
+        if self.split(m, u) and kind != 1:
+            h = RD // 2
+            slot = self.full[m].at[u, pl.ds(pl.multiple_of(s * RD + (1 - at.y_at if kind == 4 else at.y_at) * h, h), h), :]
+        peer = (at.x, at.core, at.core, at.y, at.core)[kind]
+        return remote(slot, slot, self.sems.at[0, kind, u, m], self.sems.at[1, kind, u, m], peer)
 
     def send(self, u):
-        for m in range(2):
+        for m in (1, 0) if self.split(1, u) else (0, 1):
             slot = self.slot(m, u, self.at.s)
             pltpu.make_async_copy(slot, slot, self.own.at[u, m]).wait()
             self.copy(0, m, u).start()
@@ -96,14 +105,22 @@
     def forward(self, u, m):
         self.copy(0, m, u).wait_recv()
         self.copy(2, m, u).start()
+        if self.split(m, u):
+            self.copy(3, m, u).start()
+
+    def forward_other(self, u):
+        self.copy(3, 1, u).wait_recv()
+        self.copy(4, 1, u).start()
 
     def ready(self, u, m):
         self.copy(1, m, u).wait_recv()
         self.copy(2, m, u).wait_recv()
+        if self.split(m, u):
+            self.copy(4, m, u).wait_recv()
 
     def finish(self, u):
         for m in range(2):
-            for kind in range(3):
+            for kind in range(5 if self.split(m, u) else 3):
                 self.copy(kind, m, u).wait_send()
 
 
@@ -112,7 +129,7 @@
         pltpu.VMEM((units, D, 2 * F), bf16),
         pltpu.VMEM((units, F, D), bf16),
         DMA((units, 2)),
-        DMA((2, 3, units, 2)),
+        DMA((2, 5, units, 2)),
     ]
 
 
@@ -199,13 +216,13 @@
         out[rows(c, RD), :] = value
 
 
-def forward_kernel(x, dy, sg, su, sd, h1_out, a0_out, dyt_out, gout, uout, wgu1, wd1, wd0, h1, a0, acc, xb, yb, gb, ub, sems, wgu, wd, own, gsems, osem, xsem, ysem):
+def forward_kernel(x, dy, sg, su, sd, h1_out, a0_out, dyt_out, gout, uout, wgu1, wd1, wd0, h1, a0, acc, xb, yb, gb, ub, acts, sems, wgu, wd, own, gsems, osem, xsem, ysem):
     at = Place()
-    w = Gather(at, (wgu, wd), (sg, su, sd), own, gsems)
+    w = Gather(at, (wgu, wd), (sg, su, sd), own, gsems, True)
     w.fetch(0, 0, 0)
     xs = [pltpu.make_async_copy(x.at[pl.ds(t * T, T), :], xb.at[pl.ds(t * T, T), :], xsem.at[t]) for t in range(NT)]
     xs[0].start()
-    greet((at.core, at.x))
+    greet((at.core, at.x, at.y))
     w.send(0)
     for u in range(1, EARLY):
         w.fetch(u, u // C, u % C)
@@ -236,40 +253,56 @@
     def keep(buf, out, k, i):
         return pltpu.make_async_copy(buf.at[i % 2], out.at[i // NT, :, tile(i % NT)], sems.at[k, i % 2])
 
-    for m in range(2):
-        w.forward(0, m)
-        w.ready(0, m)
-
-    def step(i, _):
-        c, t = i // NT, i % NT
-
-        @pl.when((t == 0) & (c >= 1))
-        def _():
-            w.ready(c, 0)
-            w.ready(c, 1)
-
-        @pl.when(t == NT - 1)
-        def _():
-            w.forward(c + 1, 0)
-            w.forward(c + 1, 1)
-
-        @pl.when(i >= 2)
-        def _():
-            keep(gb, gout, 0, i).wait()
-            keep(ub, uout, 1, i).wait()
-
+    def activation(i, c, t):
         both = dg(wgu[c], a0[:, tile(t)], 0, 0)
         g, u = both[:F], both[F:]
         gb[i % 2] = g
         ub[i % 2] = u
         keep(gb, gout, 0, i).start()
         keep(ub, uout, 1, i).start()
-        act = (g * sigmoid(g) * u).astype(bf16)
-
-        acc[:, tile(t)] += dg(wd[c], act, 0, 0)
+        return (g * sigmoid(g) * u).astype(bf16)
+
+    w.forward(0, 0)
+    w.ready(0, 0)
+
+    def first(t, _):
+        acts[t] = activation(t, 0, t)
         return 0
 
-    lax.fori_loop(0, STEPS, step, 0)
+    lax.fori_loop(0, 2, first, 0)
+    w.forward(0, 1)
+    w.ready(0, 1)
+
+    def second(t, _):
+        acc[:, tile(t)] = dg(wd[0], acts[t], 0, 0)
+        return 0
+
+    lax.fori_loop(0, 2, second, 0)
+    w.forward(jnp.int32(1), 1)
+
+    def step(i, _):
+        c, t = i // NT, i % NT
+
+        @pl.when((t == 0) & (c >= 1))
+        def _():
+            w.ready(c, 0)
+            w.ready(c, 1)
+
+        @pl.when(t == 1)
+        def _():
+            w.forward(c + 1, 1)
+
+        @pl.when(t == NT - 1)
+        def _():
+            w.forward_other(c + 1)
+            w.forward(c + 1, 0)
+
+        keep(gb, gout, 0, i).wait()
+        keep(ub, uout, 1, i).wait()
+        acc[:, tile(t)] += dg(wd[c], activation(i, c, t), 0, 0)
+        return 0
+
+    lax.fori_loop(2, STEPS, step, 0)
 
 
     outs.append(pltpu.make_async_copy(wd.at[pl.ds(0, C)], wd0, osem.at[0, 0]))
@@ -311,7 +344,7 @@
     h1, dh, a1, acc, scales, dgu, accgu, accd, tsem, lsem, wgu, wd, own, gsems, *refs = scratch
     at = Place()
     grads = (accgu, accd)
-    w = Gather(at, (wgu, wd), (sg, su, sd), own, gsems)
+    w = Gather(at, (wgu, wd), (sg, su, sd), own, gsems, False)
     red = Reduce(at, grads, refs)
     early = EARLY - C
     loads = [
@@ -325,18 +358,17 @@
     columns(h1_in, h1, 0, 0).start()
     for copy in loads[0]:
         copy.start()
+    for t in range(1, NT):
+        columns(h1_in, h1, 0, t).start()
+    columns(dyt, dh, 1, 0).start()
     for u in range(early, C):
         w.fetch(u, 1, u)
     for t in range(1, NT):
-        columns(h1_in, h1, 0, t).start()
-    for t in range(NT):
         columns(dyt, dh, 1, t).start()
     for load in loads[1:]:
         for copy in load:
             copy.start()
     greet((at.core, at.x, at.y, at.z))
-    for u in range(early, C):
-        w.send(u)
 
     def pre(t, _):
         columns(h1_in, h1, 0, t).wait()
@@ -348,11 +380,11 @@
         return 0
 
     lax.fori_loop(0, NT, pre, 0)
+    for u in range(early, C):
+        w.send(u)
     for load in loads:
         for copy in load:
             copy.wait()
-    for t in range(NT):
-        columns(dyt, dh, 1, t).wait()
 
     outs = (gg, gu, gd)
 
@@ -395,6 +427,10 @@
         @pl.when(t == 0)
         def _():
             clear(grads, slot)
+
+        @pl.when(i < NT)
+        def _():
+            columns(dyt, dh, 1, t).wait()
 
         a = a1[:, tile(t)]
         y = dh[:, tile(t)]
@@ -472,6 +508,11 @@
 
         return one
 
+    G, U, DOWN = (0,), (1,), (2,)
+
+    def last(u, which):
+        red.last(u, put(u), which)
+
     def step(i, _):
         c, t = i // NT, i % NT
         slot = c % 2
@@ -491,26 +532,41 @@
         @pl.when((t == 0) & (c >= 1))
         def _():
             red.to_core(c, 1 - slot)
+            red.to_yz(c - 1, U)
+
+        @pl.when((t == 0) & (c >= 2))
+        def _():
+            last(c - 2, U)
 
         @pl.when(t == 0)
         def _():
             clear(grads, slot)
 
+        @pl.when((t == 1) & (c >= 1))
+        def _():
+            red.to_yz(c - 1, DOWN)
+            red.to_zy(c - 1, G)
+
+        @pl.when(((t == 1) & (c >= 1)) | (i == 2))
+        def _():
+            red.to_x(c, 1 - slot)
+
         @pl.when((t == 1) & (c >= 2))
         def _():
-            red.last(c - 2, put(c - 2))
-
-        @pl.when((t == 1) & (c >= 1))
-        def _():
-            red.to_yz(c - 1)
-
-        @pl.when(((t == 1) & (c >= 1)) | (i == 2))
-        def _():
-            red.to_x(c, 1 - slot)
+            last(c - 2, DOWN)
+
+        @pl.when((t == 2) & (c >= 1))
+        def _():
+            red.to_zy(c - 1, U)
 
         @pl.when((t == 3) & (c >= 1))
         def _():
-            red.to_zy(c - 1)
+            red.to_zy(c - 1, DOWN)
+            last(c - 1, G)
+
+        @pl.when(t == 3)
+        def _():
+            red.to_yz(c, G)
 
         @pl.when(i + 1 < STEPS)
         def _():
@@ -529,10 +585,15 @@
 
     lax.fori_loop(0, STEPS, step, 0)
     red.to_core(C, 1)
-    red.last(C - 2, put(C - 2))
-    red.to_yz(C - 1)
-    red.to_x(C, 1)
-    red.to_zy(C - 1)
+    red.to_yz(C - 1, U)
+    last(C - 2, U)
+    red.to_x(C, 1, G)
+    red.to_x(C, 1, U)
+    red.to_yz(C - 1, DOWN)
+    red.to_x(C, 1, DOWN)
+    red.to_zy(C - 1, G)
+    last(C - 2, DOWN)
+    red.to_zy(C - 1, U)
     for c in range(C - 1):
         for q in range(4):
             sq[...] += squares(gg[1, :, q * F + c * 128 : q * F + (c + 1) * 128]) + squares(gu[1, :, q * F + c * 128 : q * F + (c + 1) * 128])
@@ -543,16 +604,19 @@
     ]
     for copy in late[1]:
         copy.start()
-    red.to_yz(C, (0,))
-    red.to_yz(C, (1,))
-    red.last(C - 1, put(C - 1))
-    red.to_zy(C, (0,))
-    red.to_yz(C, (2,))
-    red.to_zy(C, (1,))
-    red.last(C, put(C), (0,))
-    red.to_zy(C, (2,))
-    red.last(C, put(C), (1,))
-    red.last(C, put(C), (2,))
+    red.to_zy(C - 1, DOWN)
+    red.to_yz(C, G)
+    last(C - 1, G)
+    last(C - 1, U)
+    red.to_yz(C, U)
+    red.to_zy(C, G)
+    last(C - 1, DOWN)
+    red.to_yz(C, DOWN)
+    red.to_zy(C, U)
+    last(C, G)
+    red.to_zy(C, DOWN)
+    last(C, U)
+    last(C, DOWN)
     for copy in late[0]:
         copy.start()
     everyone[at.s] = sq[...]
@@ -605,7 +669,8 @@
         + [S((C, F, TOK), f32)] * 2
         + [S((early, D, 2 * F), bf16), S((early, F, D), bf16), S((C, F, D), bf16)],
         scratch_shapes=[pltpu.VMEM((D, TOK), bf16)] * 2
-        + [pltpu.VMEM((D, TOK), f32), pltpu.VMEM((TOK, D), bf16), pltpu.VMEM((D, TOK), bf16), pltpu.VMEM((2, F, T), f32), pltpu.VMEM((2, F, T), f32), DMA((2, 2))]
+        + [pltpu.VMEM((D, TOK), f32), pltpu.VMEM((TOK, D), bf16), pltpu.VMEM((D, TOK), bf16)]
+        + [pltpu.VMEM((2, F, T), f32), pltpu.VMEM((2, F, T), f32), pltpu.VMEM((2, F, T), bf16), DMA((2, 2))]
         + gather_scratch(EARLY)
         + [DMA((early + 1, 2)), DMA((NT,)), DMA((3, NT))],
         compiler_params=params(0),

time: 301 us -> 297 us (0.987)
  Pallas kernels: 300 us -> 296 us
where the time goes in v3:
time: 297 us
  Pallas kernels  296 us (100%)
    pallas_call x1, Pallas kernels, step(): pl.pallas_call(top_kernel, name='top', in_specs=[ANY] * 7, out_specs=[ANY...  122 us
    pallas_call x1, Pallas kernels, step(): pl.pallas_call(bottom_kernel, name='bottom', in_specs=[ANY] * 10, out_spe...  93 us
    pallas_call x1, Pallas kernels, step(): pl.pallas_call(forward_kernel, name='forward', in_specs=[ANY] * 5, out_sp...  65.7 us
    pallas_call x1, Pallas kernels, step(): pl.pallas_call(lambda *refs: adamw_kernel(count, *refs), name='adamw', gr...  15.2 us

profile of v3, /device:TPU:0, one launch (start us, length us, event | category | flops | bytes accessed | tf_op | source)
XLA Modules:
  0.0 296.8 jit_solution(16665579847708179693)
XLA Ops:
  0.6 65.7 %forward.1 = (bf16[640,4096]{1,0:T(8,128)(2,1)}, bf16[640,4096]{1,0:T(8,128)(2,1)}, bf16[640,4096]{1,0:T(8,128)(2,1)}, f32[4,512,4096]{2,1,0:T(8,128)}, f32[4,51...) custom-call(bf16[4096,640]{1,0:T(8,128)(2,1)} %bitcast.2, ...), custom_call_target="tpu_custom_call" | custom-call | flops 32212254720 | bytes 67108864 | tf_op jit(solution)/shard_map/forward/pallas_call | solution.py:663
  66.3 122.1 %top.1 = (bf16[640,4096]{1,0:T(8,128)(2,1)}, bf16[160,2048]{1,0:T(8,128)(2,1)}, bf16[160,2048]{1,0:T(8,128)(2,1)}, bf16[512,640]{1,0:T(8,128)(2,1)}, f32[640,1024]{1,0:T(8,128)}, /*index=5*/f32[640,512]{1,0:T(8,128)}) custom-call(bf16[640,4096]{1,0:T(8,128)(2,1)} %get-tuple-element.28.h1_in, bf16[640,4096]{1,0:T(8,128)(2,1)} %get-tuple-element.29.dyt, ...), custom_call_target="tpu_custom_call" | custom-call | flops 85899345920 | bytes 67108864 | tf_op jit(solution)/shard_map/top/pallas_call | solution.py:679
  188.4 93.0 %bottom.1 = (bf16[2,160,2048]{2,1,0:T(8,128)(2,1)}, bf16[2,160,2048]{2,1,0:T(8,128)(2,1)}, bf16[2,512,640]{2,1,0:T(8,128)(2,1)}, f32[8,128]{1,0:T(8,128)}) custom-call(bf16[640,4096]{1,0:T(8,128)(2,1)} %get-tuple-element.27.a0_in, bf16[640,4096]{1,0:T(8,128)(2,1)} %get-tuple-element.32.dh_in, bf16[4,512,640]{2,1,0:T(8,128)(2,1)} %get-tuple-element.33.wd_in, ...), custom_call_target="tpu_custom_call" | custom-call | flops 42949672960 | bytes 67108864 | tf_op jit(solution)/shard_map/bottom/pallas_call | solution.py:701
  281.4 15.2 %adamw.1 = (bf16[2,160,2048]{2,1,0:T(8,128)(2,1)}, bf16[2,160,2048]{2,1,0:T(8,128)(2,1)}, bf16[2,512,640]{2,1,0:T(8,128)(2,1)}, f32[2,160,2048]{2,1,0:T(8,128)},...) custom-call(f32[8,128]{1,0:T(8,128)} %get-tuple-element.41.refs_0_, ...), custom_call_target="tpu_custom_call" | custom-call | flops 41943040 | bytes 45088768 | tf_op jit(solution)/shard_map/adamw/pallas_call | solution.py:732
